TPU v7x, 32 devices: a whole 2x2x4 slice. The times are simulated.
32 devices in a mesh: gx: 4 (over z), gy: 2 (over y), gz: 4 (over x, core).
Axes of the slice: x: 2, y: 2, z: 4, core: 2. Of those that a mesh axis runs over, the one named last changes fastest.
Arguments:
- displacement: float32 [3, 64, 64, 1024], P(None, 'gx', 'gy', 'gz'), may hold values from -1.5 to 1.5
- density: float32 [64, 64, 1024], P('gx', 'gy', 'gz'), may hold values from 0.03 to 1
- stiffness: float32 [24, 24], replicated, may hold values from -9 to 9.5, as said below
Outputs:
- filtered: float32 [64, 64, 1024], P('gx', 'gy', 'gz')
- compliance: float32 [], replicated
- volume: float32 [], replicated
Inputs may be any that keep to these rules, and one draw needn't show every extreme that they name: `stiffness`: symmetric and positive definite, every eigenvalue at least 0.5.
All inputs are finite; a program needn't handle non-finite values.
Results may differ from a plain program's by a relative error of at most 0.00005.
Values sent between devices are 32-bit elements; how exact they have to be, the bound alone decides.
No kernel may reach another device: no remote copies, remote signals or barrier semaphores. Data moves between devices by JAX's collectives and lax.ppermute only.
A program may use at most 64 MiB of HBM per device.

v0:
```python
import jax
import jax.numpy as jnp
from jax import lax
from jax.sharding import PartitionSpec as P

VOID_STIFFNESS = 0.001
KERNEL = (1.0, 2.0, 3.0, 2.0, 1.0)


def from_behind(block, axis, distance):
    devices = range(lax.axis_size(axis))
    route = [(i - distance, i) for i in devices if i - distance in devices]
    return lax.ppermute(block, axis, route)


def with_halo(shard, sides, width):
    for axis, dim in sides:
        count, length = (lax.axis_size(axis), shard.shape[dim])
        up = [(i, (i + 1) % count) for i in range(count - 1)]
        down = [(j, i) for i, j in up]
        last = lax.slice_in_dim(shard, length - width, length, axis=dim)
        first = lax.slice_in_dim(shard, 0, width, axis=dim)
        before = lax.ppermute(last, axis, up)
        after = lax.ppermute(first, axis, down)
        shard = jnp.concatenate([before, shard, after], axis=dim)
    return shard


def smooth(values, along):
    length = values.shape[along] - 4
    summed = None
    for offset in range(5):
        section = lax.slice_in_dim(values, offset, offset + length, axis=along)
        scaled = KERNEL[offset] * section
        summed = scaled if summed is None else summed + scaled
    return summed


def side_sums(first, amount, extent):
    position = first + jnp.arange(amount, dtype=jnp.int32)
    summed = jnp.zeros((amount,), jnp.float32)
    for offset in range(5):
        inside = (position + offset - 2 >= 0) & (position + offset - 2 < extent)
        summed = summed + KERNEL[offset] * inside.astype(jnp.float32)
    return summed


def plane_energy(slab_nodes, stiffness):
    height = slab_nodes.shape[2] - 1
    length = slab_nodes.shape[3] - 1
    corner_rows = jnp.stack(
        [
            slab_nodes[
                member, along_x, along_y : along_y + height, along_z : along_z + length
            ].reshape(-1)
            for member in range(3)
            for along_x in range(2)
            for along_y in range(2)
            for along_z in range(2)
        ]
    )
    product = jnp.dot(
        stiffness, corner_rows, precision=lax.Precision.HIGHEST, preferred_element_type=jnp.float32
    )
    return jnp.sum(corner_rows * product, axis=0).reshape(height, length)


def energies(node_field, stiffness, planes):

    def one_plane(plane_index):
        slab_nodes = lax.dynamic_slice_in_dim(node_field, plane_index, 2, 1)
        return plane_energy(slab_nodes, stiffness)

    return lax.map(one_plane, jnp.arange(planes, dtype=jnp.int32))


def hole_sums(cells_first, cells_second, cells_third, margin):
    first_sums = side_sums(
        lax.axis_index("gx") * cells_first - margin,
        cells_first + 2 * margin,
        cells_first * lax.axis_size("gx"),
    )
    second_sums = side_sums(
        lax.axis_index("gy") * cells_second - margin,
        cells_second + 2 * margin,
        cells_second * lax.axis_size("gy"),
    )
    third_sums = side_sums(
        lax.axis_index("gz") * cells_third - margin,
        cells_third + 2 * margin,
        cells_third * lax.axis_size("gz"),
    )
    return first_sums[:, None, None] * second_sums[None, :, None] * third_sums[None, None, :]


def on_device(displacement, density, stiffness):
    cells_first, cells_second, cells_third = density.shape
    modulus = VOID_STIFFNESS + density * density * density * (1.0 - VOID_STIFFNESS)
    node_field = displacement
    upper_layer = from_behind(node_field[:, :1], "gx", -1)
    node_field = jnp.concatenate([node_field, upper_layer], axis=1)
    upper_layer = from_behind(node_field[:, :, :1], "gy", -1)
    node_field = jnp.concatenate([node_field, upper_layer], axis=2)
    upper_layer = from_behind(node_field[:, :, :, :1], "gz", -1)
    node_field = jnp.concatenate([node_field, upper_layer], axis=3)
    energy = energies(node_field, stiffness, cells_first)
    sensitivity = -3.0 * (1.0 - VOID_STIFFNESS) * density * density * energy
    weighted = sensitivity / hole_sums(cells_first, cells_second, cells_third, 0)
    spread = with_halo(weighted, (("gx", 0), ("gy", 1), ("gz", 2)), 2)
    filtered = smooth(smooth(smooth(spread, 0), 1), 2)
    totals = lax.psum((jnp.sum(modulus * energy), jnp.sum(density)), ("gx", "gy", "gz"))
    cell_count = float(
        cells_first
        * cells_second
        * cells_third
        * lax.axis_size("gx")
        * lax.axis_size("gy")
        * lax.axis_size("gz")
    )
    return (filtered, totals[0] / cell_count, totals[1] / cell_count)


def solution(mesh):
    return jax.shard_map(
        on_device,
        mesh=mesh,
        in_specs=(P(None, "gx", "gy", "gz"), P("gx", "gy", "gz"), P()),
        out_specs=(P("gx", "gy", "gz"), P(), P()),
        check_vma=False,
    )
```

profile of v0, /device:TPU:1, one launch (start us, length us, event | category | flops | bytes accessed | tf_op | source)
XLA Modules:
  0.0 205.5 jit_solution(15581065391671610939)
XLA Ops:
  4.4 3.6 %collective-permute-done = f32[3,1,32,256]{3,2,1,0:T(8,128)S(1)} collective-permute-done((f32[3,1,32,256]{3,2,1,0:T(8,128)S(1)}, f32[3,1,32,256]{3,2,1,0:T(8,128)S(1)}, u32[]{:S(2)}, u32[]{:S(2)}) %collective-permute-start) | collective-permute-done | bytes 98336 | tf_op jit(solution)/shard_map/ppermute | solution.py:13
  9.5 3.5 %collective-permute-done.1 = f32[3,17,1,256]{3,2,1,0:T(1,128)S(1)} collective-permute-done((f32[3,17,1,256]{3,2,1,0:T(1,128)S(1)}, f32[3,17,1,256]{3,2,1,0:T(1,128)S(1)}, u32[]{:S(2)}, u32[]{:S(2)}) %collective-permute-start.1) | collective-permute-done | bytes 52256 | tf_op jit(solution)/shard_map/ppermute | solution.py:13
  13.5 4.3 %collective-permute-start.2 = (f32[3,17,33,1]{2,3,1,0:T(1,128)S(1)}, f32[3,17,33,1]{2,3,1,0:T(1,128)S(1)}, u32[]{:S(2)}, u32[]{:S(2)}) collective-permute-start(f32[3,17,33,1]{2,3,1,0:T(1,128)S(1)} %copy.11), channel_id=1, source_target_pairs={{1,0},{2,1},{3,2},{5,4},{6,5},{7,6},{9,8},{10,9},{11,10},{13,12},{... | collective-permute-start | bytes 20204 | tf_op jit(solution)/shard_map/ppermute | solution.py:13
  17.8 2.8 %collective-permute-done.2 = f32[3,17,33,1]{2,3,1,0:T(1,128)S(1)} collective-permute-done((f32[3,17,33,1]{2,3,1,0:T(1,128)S(1)}, f32[3,17,33,1]{2,3,1,0:T(1,128)S(1)}, u32[]{:S(2)}, u32[]{:S(2)}) %collective-permute-start.2) | collective-permute-done | bytes 6764 | tf_op jit(solution)/shard_map/ppermute | solution.py:13
  21.1 1.9 pad_maximum_fusion
  23.0 115.6 %while.10 = (s32[]{:T(128)}, f32[16,32,256]{2,1,0:T(8,128)S(1)}, s32[16]{0:T(128)S(1)}, f32[3,17,33,257]{3,2,1,0:T(8,128)}, f32[24,24]{1,0:T(8,128)S(1)}, /*index=5*/s32[]{:T(128)}, s32[]{:T(128)}, s32[]{}, s32[]{:T(128)}, s32[]{}) while((s32[]{:T(128)}, f32[16,32,256]{2,1,0:T(8,128)S(1)}, s32[16]{0:T(128)S(1)}, f32[3,17,33,257]{3,2,1,0:T(8,128)}, ...), condition=%wide.region_2.3_spmd, body=%wide.region_0.2_spmd.sunk | while | flops 57008136 | bytes 5671371 | solution.py:74
  25.6 1.6 dynamic-slice_bitcast_fusion.25
  32.8 1.7 dynamic-slice_bitcast_fusion.25
  40.0 1.6 dynamic-slice_bitcast_fusion.25
  68.7 1.7 dynamic-slice_bitcast_fusion.25
  76.0 1.6 dynamic-slice_bitcast_fusion.25
  83.3 1.6 dynamic-slice_bitcast_fusion.25
  97.7 1.6 dynamic-slice_bitcast_fusion.25
  104.9 1.6 dynamic-slice_bitcast_fusion.25
  112.1 1.6 dynamic-slice_bitcast_fusion.25
  119.3 1.7 dynamic-slice_bitcast_fusion.25
  126.7 1.6 dynamic-slice_bitcast_fusion.25
  133.9 1.7 dynamic-slice_bitcast_fusion.25
  139.4 3.2 %collective-permute-start.3 = (f32[2,32,256]{2,1,0:T(8,128)S(1)}, f32[2,32,256]{2,1,0:T(8,128)S(1)}, u32[]{:S(2)}, u32[]{:S(2)}) collective-permute-start(f32[2,32,256]{2,1,0:T(8,128)S(1)} %get-tuple-element.79), channel_id=1, source_target_pairs={{0,8},{8,16},{16,24},{1,9},{9,17},{17,25},{2,10},{10,18},{18,26},{... | collective-permute-start | bytes 196616 | tf_op jit(solution)/shard_map/ppermute | solution.py:23
  144.0 3.7 %collective-permute-done.4 = f32[2,32,256]{2,1,0:T(8,128)S(1)} collective-permute-done((f32[2,32,256]{2,1,0:T(8,128)S(1)}, f32[2,32,256]{2,1,0:T(8,128)S(1)}, u32[]{:S(2)}, u32[]{:S(2)}) %collective-permute-start.4) | collective-permute-done | bytes 65568 | tf_op jit(solution)/shard_map/ppermute | solution.py:24
  150.3 3.4 %collective-permute-done.6 = f32[20,2,256]{2,1,0:T(2,128)S(1)} collective-permute-done((f32[20,2,256]{2,1,0:T(2,128)S(1)}, f32[20,2,256]{2,1,0:T(2,128)S(1)}, u32[]{:S(2)}, u32[]{:S(2)}) %collective-permute-start.6) | collective-permute-done | bytes 40992 | tf_op jit(solution)/shard_map/ppermute | solution.py:24
  154.0 4.8 %collective-permute-start.7 = (f32[20,36,2]{2,1,0:T(8,128)S(1)}, f32[20,36,2]{2,1,0:T(8,128)S(1)}, u32[]{:S(2)}, u32[]{:S(2)}) collective-permute-start(f32[20,36,2]{2,1,0:T(8,128)S(1)} %get-tuple-element.75), channel_id=1, source_target_pairs={{0,1},{1,2},{2,3},{4,5},{5,6},{6,7},{8,9},{9,10},{10,11},{12,13},{... | collective-permute-start | bytes 17288 | tf_op jit(solution)/shard_map/ppermute | solution.py:23
  158.8 1.9 collective-permute-start.8
  160.8 38.5 %all-reduce = (f32[]{:T(128)}, f32[]{:T(128)}) all-reduce(f32[]{:T(128)} %get-tuple-element.37, f32[]{:T(128)} %get-tuple-element.36), channel_id=1, replica_groups=mesh['gx'=4,'gy'=2,'gz'=4] {'gx','gy','gz'}, use_global_device_ids=true, to_apply=%region_4.5 | all-reduce | flops 2 | bytes 16 | tf_op jit(solution)/shard_map/psum | solution.py:111
  (503 shorter events, 74.9 us)
Async XLA Ops:
  1.5 6.5 %collective-permute-start = (f32[3,1,32,256]{3,2,1,0:T(8,128)S(1)}, f32[3,1,32,256]{3,2,1,0:T(8,128)S(1)}, u32[]{:S(2)}, u32[]{:S(2)}) collective-permute-start(f32[3,1,32,256]{3,2,1,0:T(8,128)S(1)} %slice.144), channel_id=1, source_target_pairs={{8,0},{16,8},{24,16},{9,1},{17,9},{25,17},{10,2},{18,10},{26,18},{... | collective-permute-start | bytes 294920 | tf_op jit(solution)/shard_map/ppermute | solution.py:13
  8.1 4.9 %collective-permute-start.1 = (f32[3,17,1,256]{3,2,1,0:T(1,128)S(1)}, f32[3,17,1,256]{3,2,1,0:T(1,128)S(1)}, u32[]{:S(2)}, u32[]{:S(2)}) collective-permute-start(f32[3,17,1,256]{3,2,1,0:T(1,128)S(1)} %slice.168), channel_id=1, source_target_pairs={{4,0},{5,1},{6,2},{7,3},{12,8},{13,9},{14,10},{15,11},{20,16},{21,... | collective-permute-start | bytes 156680 | tf_op jit(solution)/shard_map/ppermute | solution.py:13
  13.5 7.2 %collective-permute-start.2 = (f32[3,17,33,1]{2,3,1,0:T(1,128)S(1)}, f32[3,17,33,1]{2,3,1,0:T(1,128)S(1)}, u32[]{:S(2)}, u32[]{:S(2)}) collective-permute-start(f32[3,17,33,1]{2,3,1,0:T(1,128)S(1)} %copy.11), channel_id=1, source_target_pairs={{1,0},{2,1},{3,2},{5,4},{6,5},{7,6},{9,8},{10,9},{11,10},{13,12},{... | collective-permute-start | bytes 20204 | tf_op jit(solution)/shard_map/ppermute | solution.py:13
  21.1 1.9 copy-start.1
  23.0 115.6 %copy-start = (f32[16,32,256]{2,1,0:T(8,128)S(1)}, f32[16,32,256]{2,1,0:T(8,128)}, u32[]{:S(2)}) copy-start(f32[16,32,256]{2,1,0:T(8,128)} %param.6) | copy-start | bytes 1572868
  139.4 4.5 %collective-permute-start.3 = (f32[2,32,256]{2,1,0:T(8,128)S(1)}, f32[2,32,256]{2,1,0:T(8,128)S(1)}, u32[]{:S(2)}, u32[]{:S(2)}) collective-permute-start(f32[2,32,256]{2,1,0:T(8,128)S(1)} %get-tuple-element.79), channel_id=1, source_target_pairs={{0,8},{8,16},{16,24},{1,9},{9,17},{17,25},{2,10},{10,18},{18,26},{... | collective-permute-start | bytes 196616 | tf_op jit(solution)/shard_map/ppermute | solution.py:23
  142.6 5.0 %collective-permute-start.4 = (f32[2,32,256]{2,1,0:T(8,128)S(1)}, f32[2,32,256]{2,1,0:T(8,128)S(1)}, u32[]{:S(2)}, u32[]{:S(2)}) collective-permute-start(f32[2,32,256]{2,1,0:T(8,128)S(1)} %get-tuple-element.80), channel_id=1, source_target_pairs={{8,0},{16,8},{24,16},{9,1},{17,9},{25,17},{10,2},{18,10},{26,18},{... | collective-permute-start | bytes 196616 | tf_op jit(solution)/shard_map/ppermute | solution.py:24
  147.7 2.6 %collective-permute-start.5 = (f32[20,2,256]{2,1,0:T(2,128)S(1)}, f32[20,2,256]{2,1,0:T(2,128)S(1)}, u32[]{:S(2)}, u32[]{:S(2)}) collective-permute-start(f32[20,2,256]{2,1,0:T(2,128)S(1)} %get-tuple-element.77), channel_id=1, source_target_pairs={{0,4},{1,5},{2,6},{3,7},{8,12},{9,13},{10,14},{11,15},{16,20},{17,... | collective-permute-start | bytes 122888 | tf_op jit(solution)/shard_map/ppermute | solution.py:23
  149.0 4.7 %collective-permute-start.6 = (f32[20,2,256]{2,1,0:T(2,128)S(1)}, f32[20,2,256]{2,1,0:T(2,128)S(1)}, u32[]{:S(2)}, u32[]{:S(2)}) collective-permute-start(f32[20,2,256]{2,1,0:T(2,128)S(1)} %get-tuple-element.78), channel_id=1, source_target_pairs={{4,0},{5,1},{6,2},{7,3},{12,8},{13,9},{14,10},{15,11},{20,16},{21,... | collective-permute-start | bytes 122888 | tf_op jit(solution)/shard_map/ppermute | solution.py:24
  154.0 46.5 %collective-permute-start.7 = (f32[20,36,2]{2,1,0:T(8,128)S(1)}, f32[20,36,2]{2,1,0:T(8,128)S(1)}, u32[]{:S(2)}, u32[]{:S(2)}) collective-permute-start(f32[20,36,2]{2,1,0:T(8,128)S(1)} %get-tuple-element.75), channel_id=1, source_target_pairs={{0,1},{1,2},{2,3},{4,5},{5,6},{6,7},{8,9},{9,10},{10,11},{12,13},{... | collective-permute-start | bytes 17288 | tf_op jit(solution)/shard_map/ppermute | solution.py:23
  158.8 41.7 %collective-permute-start.8 = (f32[20,36,2]{2,1,0:T(8,128)S(1)}, f32[20,36,2]{2,1,0:T(8,128)S(1)}, u32[]{:S(2)}, u32[]{:S(2)}) collective-permute-start(f32[20,36,2]{2,1,0:T(8,128)S(1)} %get-tuple-element.76), channel_id=1, source_target_pairs={{1,0},{2,1},{3,2},{5,4},{6,5},{7,6},{9,8},{10,9},{11,10},{13,12},{... | collective-permute-start | bytes 17288 | tf_op jit(solution)/shard_map/ppermute | solution.py:24
where the time goes:
time: 209 us; the launch traced here: 205 us
  local copies, waits for them, and re-layouts  71 us (34%)
  blocking collectives  38.5 us (18%)
  loops' own time  35 us (17%)
  starting transfers between devices  20.7 us (10%)
  waiting for transfers between devices  17.1 us (8%)
  matrix products  13.2 us (6%)
  other arithmetic  5.63 us (3%)
  between operations  4.4 us (2%)
    while x400, local copies, waits for them, and re-layouts  39.2 us
    psum x1, blocking collectives, on_device(): lax.psum((jnp.sum(modulus * energy), jnp.sum(density)), ('gx', 'gy', 'gz'))  38.5 us
    another operation x1, loops' own time, energies(): return lax.map(one_plane, jnp.arange(planes, dtype=jnp.int32))  35 us
    another operation x16, local copies, waits for them, and re-layouts, plane_energy(): jnp.stack([slab_nodes[member, along_x, along_y:along_y + height, along_z:...  18.5 us
    dot_general x16, matrix products, plane_energy(): jnp.dot(stiffness, corner_rows, precision=lax.Precision.HIGHEST, preferre...  13.2 us
    ppermute x3, waiting for transfers between devices, from_behind(): return lax.ppermute(block, axis, route)  9.96 us
    dynamic_slice x16, local copies, waits for them, and re-layouts, energies(): return lax.map(one_plane, jnp.arange(planes, dtype=jnp.int32))  9.38 us
    ppermute x3, starting transfers between devices, with_halo(): before = lax.ppermute(last, axis, up)  9.28 us
  transfers between devices with their start and end apart: 9, of which 5 were waited for; matrix products, arithmetic and copies ran while one was open for 1% of the time, Pallas kernels for 0%

commit v1 on v0

v1 whole, which is shorter than its diff:
```python
import functools

import jax
import jax.numpy as jnp
from jax import lax
from jax.experimental import pallas as pl
from jax.experimental.pallas import tpu as pltpu
from jax.sharding import PartitionSpec as P

VOID = 0.001
AXES = ("gx", "gy", "gz")
F32 = jnp.float32
BF16 = jnp.bfloat16
LANES = 128
ROWS = 8


def shift_from(block, axis, distance):
    count = lax.axis_size(axis)
    route = [(i + distance, i) for i in range(count) if 0 <= i + distance < count]
    return lax.ppermute(block, axis, route)


def both_sides(low_part, high_part, axis):
    count = lax.axis_size(axis)
    if count == 2:
        at = lax.axis_index(axis)
        got = lax.ppermute(jnp.where(at == 0, high_part, low_part), axis, [(0, 1), (1, 0)])
        zero = jnp.zeros_like(got)
        return jnp.where(at == 1, got, zero), jnp.where(at == 0, got, zero)
    return shift_from(high_part, axis, -1), shift_from(low_part, axis, 1)


def missing(position, extent):
    lost = (
        3.0 * (position == 0).astype(F32)
        + 1.0 * (position == 1).astype(F32)
        + 3.0 * (position == extent - 1).astype(F32)
        + 1.0 * (position == extent - 2).astype(F32)
    )
    return 9.0 - lost


def energy_kernel(
    where_ref, u_ref, xh_ref, yh_ref, zh_ref, rho_ref, k_ref, w_ref, sums_ref, corners, gains, inv_ref,
    *, extents
):
    planes, height, length = rho_ref.shape
    side = 24 * ROWS

    k = k_ref[...]
    k_hi = k.astype(BF16)
    k_lo = (k - k_hi.astype(F32)).astype(BF16)
    r0 = lax.broadcasted_iota(jnp.int32, (side, 24), 0)
    r1 = lax.broadcasted_iota(jnp.int32, (side, 24), 1)
    spread = (r0 // ROWS == r1).astype(F32).astype(BF16)
    d0 = lax.broadcasted_iota(jnp.int32, (side, side), 0)
    d1 = lax.broadcasted_iota(jnp.int32, (side, side), 1)
    same_row = (d0 % ROWS) == (d1 % ROWS)
    for part, kk in enumerate((k_hi, k_lo)):
        tall = jnp.dot(spread, kk, preferred_element_type=F32).astype(BF16)
        full = lax.dot_general(tall, spread, (((1,), (1,)), ((), ())), preferred_element_type=F32)
        gains[part * side : (part + 1) * side, :] = jnp.where(same_row, full, 0.0).astype(BF16)

    row = lax.broadcasted_iota(jnp.int32, (height, length), 0)
    lane = lax.broadcasted_iota(jnp.int32, (height, length), 1)
    second = missing(row + where_ref[1] * height, extents[1])
    third = missing(lane + where_ref[2] * length, extents[2])
    inv_ref[...] = (-3.0 * (1.0 - VOID)) / (second * third)
    last_row = row == height - 1
    last_lane = lane == length - 1

    def prepare(plane_of, p, slot):
        turned = zh_ref[p].T
        for m in range(3):
            plane = plane_of(m)
            col0 = turned[0:height, m : m + 1]
            col1 = turned[0:height, m + 4 : m + 5]
            up = jnp.where(last_row, yh_ref[m, pl.ds(p, 1), :], pltpu.roll(plane, height - 1, 0))
            corners[slot, 4 * m + 0] = plane
            corners[slot, 4 * m + 1] = jnp.where(last_lane, col0, pltpu.roll(plane, length - 1, 1))
            corners[slot, 4 * m + 2] = up
            corners[slot, 4 * m + 3] = jnp.where(last_lane, col1, pltpu.roll(up, length - 1, 1))

    prepare(lambda m: u_ref[m, 0], 0, 0)

    def element_plane(i, slot, nxt, sums):
        total, amount = sums
        first = missing(where_ref[0] * planes + i + jnp.zeros((ROWS, length), jnp.int32), extents[0])
        inv_first = 1.0 / first
        for j in range(height // ROWS):
            rows = slice(j * ROWS, (j + 1) * ROWS)
            x = jnp.concatenate(
                [
                    corners[(slot, nxt)[a], 4 * m + 2 * b + c, rows, :]
                    for m in range(3)
                    for a in range(2)
                    for b in range(2)
                    for c in range(2)
                ],
                axis=0,
            )
            h = x.astype(BF16)
            y = jnp.dot(gains[...], h, preferred_element_type=F32)
            y = y[:side] + y[side:]
            e = ((2.0 * x - h.astype(F32)) * y).reshape(24, ROWS, length).sum(axis=0)
            rho = rho_ref[i, rows, :]
            square = rho * rho
            w_ref[i, rows, :] = square * e * (inv_ref[rows, :] * inv_first)
            total = total + (VOID + square * rho * (1.0 - VOID)) * e
            amount = amount + rho
        return total, amount

    def step(i, sums):
        slot = lax.rem(i, 2)
        prepare(lambda m: u_ref[m, i + 1], i + 1, 1 - slot)
        return element_plane(i, slot, 1 - slot, sums)

    zero = jnp.zeros((ROWS, length), F32)
    sums = lax.fori_loop(0, planes - 1, step, (zero, zero))
    slot = (planes - 1) % 2
    prepare(lambda m: xh_ref[m, 0], planes, 1 - slot)
    total, amount = element_plane(planes - 1, slot, 1 - slot, sums)
    at = lax.broadcasted_iota(jnp.int32, sums_ref.shape, 1)
    sums_ref[...] = jnp.where(at == 0, jnp.sum(total), jnp.where(at == 1, jnp.sum(amount), 0.0))


def filter_kernel(w_ref, xlo_ref, xhi_ref, ylo_ref, yhi_ref, z_ref, out_ref, field):
    planes, height, length = w_ref.shape
    full_rows, full_lanes = field.shape[1:]

    def fill(p, body):
        field[p, 0:height, 0:length] = body
        tail = jnp.concatenate(
            [yhi_ref[p], jnp.zeros((ROWS - 4, length), F32), ylo_ref[p]], axis=0
        )
        field[p, height : height + ROWS, 0:length] = tail
        z = z_ref[p]
        block = jnp.concatenate([z[0:2], jnp.zeros((LANES - 4, LANES), F32), z[2:4]], axis=0)
        field[p, :, length : length + LANES] = block.T[0:full_rows]

    def box(v, axis):
        n = v.shape[axis]
        return v + pltpu.roll(v, 1, axis) + pltpu.roll(v, n - 1, axis)

    for p in range(2):
        fill(p, xlo_ref[p])
        fill(planes + 2 + p, xhi_ref[p])

    def middle(p, carry):
        fill(p + 2, w_ref[p])
        return carry

    lax.fori_loop(0, planes, middle, 0)

    def one(i, carry):
        a, b, c, d, e = (field[i + k] for k in range(5))
        t = (a + e) + 2.0 * (b + d) + 3.0 * c
        t = box(box(t, 0), 0)[0:height]
        t = box(box(t, 1), 1)
        out_ref[i] = t[:, 0:length]
        return carry

    lax.fori_loop(0, planes, one, 0)


VMEM = pl.BlockSpec(memory_space=pltpu.VMEM)
SMEM = pl.BlockSpec(memory_space=pltpu.SMEM)


def on_device(displacement, density, stiffness):
    planes, height, length = density.shape
    sizes = tuple(lax.axis_size(a) for a in AXES)
    devices = sizes[0] * sizes[1] * sizes[2]
    extents = tuple(n * s for n, s in zip(density.shape, sizes))
    where = jnp.stack([lax.axis_index(a) for a in AXES]).astype(jnp.int32)

    xh = shift_from(displacement[:, :1], "gx", 1)
    yrow = jnp.concatenate([displacement[:, :, 0], xh[:, :, 0]], axis=1)
    yh = shift_from(yrow, "gy", 1)
    zcol = jnp.concatenate([displacement[..., 0], xh[..., 0]], axis=1)
    zcol = jnp.concatenate([zcol, yh[..., :1]], axis=2)
    zh = shift_from(zcol.transpose(1, 0, 2), "gz", 1)
    gap = LANES - height
    zh = jnp.concatenate(
        [
            jnp.pad(zh[..., :height], ((0, 0), (0, 1), (0, gap))),
            jnp.pad(zh[..., 1:], ((0, 0), (0, 1), (0, gap))),
        ],
        axis=1,
    )

    weighted, sums = pl.pallas_call(
        functools.partial(energy_kernel, extents=extents),
        in_specs=[SMEM] + [VMEM] * 6,
        out_specs=[VMEM, VMEM],
        out_shape=[
            jax.ShapeDtypeStruct(density.shape, F32),
            jax.ShapeDtypeStruct((devices, LANES), F32),
        ],
        scratch_shapes=[
            pltpu.VMEM((2, 12, height, length), F32),
            pltpu.VMEM((48 * ROWS, 24 * ROWS), BF16),
            pltpu.VMEM((height, length), F32),
        ],
        name="energy",
    )(where, displacement, xh, yh, zh, density, stiffness)

    gathered = lax.all_to_all(sums, AXES, 0, 0, tiled=True)
    totals = jnp.sum(gathered, axis=0)

    xlo, xhi = both_sides(weighted[:2], weighted[-2:], "gx")
    low = jnp.concatenate([v[:, :2] for v in (xlo, weighted, xhi)], axis=0)
    high = jnp.concatenate([v[:, -2:] for v in (xlo, weighted, xhi)], axis=0)
    ylo, yhi = both_sides(low, high, "gy")

    def columns(part):
        middle = jnp.concatenate([v[..., part] for v in (xlo, weighted, xhi)], axis=0)
        gap = jnp.zeros((planes + 4, ROWS - 4, 2), F32)
        whole = jnp.concatenate([middle, yhi[..., part], gap, ylo[..., part]], axis=1)
        return whole.transpose(0, 2, 1)

    zlo, zhi = both_sides(columns(slice(0, 2)), columns(slice(length - 2, length)), "gz")
    z = jnp.pad(jnp.concatenate([zhi, zlo], axis=1), ((0, 0), (0, 4), (0, LANES - height - ROWS)))

    filtered = pl.pallas_call(
        filter_kernel,
        in_specs=[VMEM] * 6,
        out_specs=VMEM,
        out_shape=jax.ShapeDtypeStruct(density.shape, F32),
        scratch_shapes=[pltpu.VMEM((planes + 4, height + ROWS, length + LANES), F32)],
        name="cone",
    )(weighted, xlo, xhi, ylo, yhi, z)

    cells = float(extents[0] * extents[1] * extents[2])
    return filtered, totals[0] / cells, totals[1] / cells


def solution(mesh):
    return jax.shard_map(
        on_device,
        mesh=mesh,
        in_specs=(P(None, *AXES), P(*AXES), P()),
        out_specs=(P(*AXES), P(), P()),
        check_vma=False,
    )
```

time: 209 us -> 90.3 us (0.43); the launches traced: 205 us -> 89.6 us
  local copies, waits for them, and re-layouts: 71 us -> 22.2 us
  blocking collectives: 38.5 us -> 0 us
  loops' own time: 35 us -> 0 us
  Pallas kernels: 0 us -> 19.1 us
  matrix products: 13.2 us -> 0 us
  waiting for transfers between devices: 17.1 us -> 13.4 us
  starting transfers between devices: 20.7 us -> 24.1 us
    while x400 -> x0, local copies, waits for them, and re-layouts: 39.2 us -> none
    psum x1 -> x0, blocking collectives: 38.5 us -> none  [on_device(): lax.psum((jnp.sum(modulus * energy), jnp.sum(density)), ('gx', 'gy', 'gz'))]
    another operation x1 -> x0, loops' own time: 35 us -> none  [energies(): return lax.map(one_plane, jnp.arange(planes, dtype=jnp.int32))]
    pallas_call x0 -> x2, Pallas kernels: none -> 19.1 us  [the longest x1 12.4 us: on_device(): pl.pallas_call(functools.partial(energy_kernel, extents=extents), in_spec...]
    another operation x16 -> x1, local copies, waits for them, and re-layouts: 18.5 us -> 0.01 us  [plane_energy(): jnp.stack([slab_nodes[member, along_x, along_y:along_y + height, along_z:...]
    dot_general x16 -> x0, matrix products: 13.2 us -> none  [plane_energy(): jnp.dot(stiffness, corner_rows, precision=lax.Precision.HIGHEST, preferre...]
    dynamic_slice x16 -> x0, local copies, waits for them, and re-layouts: 9.38 us -> none  [energies(): return lax.map(one_plane, jnp.arange(planes, dtype=jnp.int32))]
    slice x4 -> x19, local copies, waits for them, and re-layouts: 1.11 us -> 8.09 us  [the longest x4 3.21 us: on_device(): low = jnp.concatenate([v[:, :2] for v in (xlo, weighted, xhi)], axis=0)]
  transfers between devices with their start and end apart: 9 -> 9, of which waited for: 5 -> 6; matrix products, arithmetic and copies ran while one was open for 1% -> 16% of each run, Pallas kernels for 0% -> 0%
where the time goes in v1:
time: 90.3 us; the launch traced here: 89.6 us
  starting transfers between devices  24.1 us (27%)
  local copies, waits for them, and re-layouts  22.2 us (25%)
  Pallas kernels  19.1 us (21%)
  waiting for transfers between devices  13.4 us (15%)
  other arithmetic  6.41 us (7%)
  between operations  4.4 us (5%)
    ppermute x7, starting transfers between devices, shift_from(): return lax.ppermute(block, axis, route)  19.8 us
    pallas_call x1, Pallas kernels, on_device(): pl.pallas_call(functools.partial(energy_kernel, extents=extents), in_spec...  12.4 us
    ppermute x7, waiting for transfers between devices, shift_from(): return lax.ppermute(block, axis, route)  11.8 us
    pallas_call x1, Pallas kernels, on_device(): pl.pallas_call(filter_kernel, in_specs=[VMEM] * 6, out_specs=VMEM, out_sh...  6.68 us
    select_n x2, local copies, waits for them, and re-layouts, both_sides(): return (jnp.where(at == 1, got, zero), jnp.where(at == 0, got, zero))  4.5 us
    slice x4, local copies, waits for them, and re-layouts, on_device(): low = jnp.concatenate([v[:, :2] for v in (xlo, weighted, xhi)], axis=0)  3.21 us
    all_to_all x1, starting transfers between devices, on_device(): gathered = lax.all_to_all(sums, AXES, 0, 0, tiled=True)  3.03 us
    ppermute x4, local copies, waits for them, and re-layouts, shift_from(): return lax.ppermute(block, axis, route)  2.78 us
  transfers between devices with their start and end apart: 9, of which 6 were waited for; matrix products, arithmetic and copies ran while one was open for 16% of the time, Pallas kernels for 0%

profile of v1, /device:TPU:1, one launch (start us, length us, event | category | flops | bytes accessed | tf_op | source)
XLA Modules:
  0.0 89.6 jit_solution(5323344609553992496)
XLA Ops:
  1.7 1.3 %collective-permute-start = (f32[3,1,32,256]{3,0,2,1:T(4,128)S(1)}, f32[3,1,32,256]{3,0,2,1:T(4,128)S(1)}, u32[]{:S(2)}, u32[]{:S(2)}) collective-permute-start(f32[3,1,32,256]{3,0,2,1:T(4,128)S(1)} %copy.69), channel_id=1, source_target_pairs={{8,0},{16,8},{24,16},{9,1},{17,9},{25,17},{10,2},{18,10},{26,18},{... | collective-permute-start | bytes 294920 | tf_op jit(solution)/shard_map/ppermute | solution.py:21
  4.1 4.8 %collective-permute-done = f32[3,1,32,256]{3,0,2,1:T(4,128)S(1)} collective-permute-done((f32[3,1,32,256]{3,0,2,1:T(4,128)S(1)}, f32[3,1,32,256]{3,0,2,1:T(4,128)S(1)}, u32[]{:S(2)}, u32[]{:S(2)}) %collective-permute-start) | collective-permute-done | bytes 98336 | tf_op jit(solution)/shard_map/ppermute | solution.py:21
  8.9 1.3 %collective-permute-start.1 = (f32[3,17,256]{2,0,1:T(4,128)S(1)}, f32[3,17,256]{2,0,1:T(4,128)S(1)}, u32[]{:S(2)}, u32[]{:S(2)}) collective-permute-start(f32[3,17,256]{2,0,1:T(4,128)S(1)} %pad_maximum_fusion), channel_id=1, source_target_pairs={{4,0},{5,1},{6,2},{7,3},{12,8},{13,9},{14,10},{15,11},{20,16},{21,... | collective-permute-start | bytes 156680 | tf_op jit(solution)/shard_map/ppermute | solution.py:21
  10.8 3.2 %collective-permute-done.1 = f32[3,17,256]{2,0,1:T(4,128)S(1)} collective-permute-done((f32[3,17,256]{2,0,1:T(4,128)S(1)}, f32[3,17,256]{2,0,1:T(4,128)S(1)}, u32[]{:S(2)}, u32[]{:S(2)}) %collective-permute-start.1) | collective-permute-done | bytes 52256 | tf_op jit(solution)/shard_map/ppermute | solution.py:21
  14.1 4.3 %collective-permute-start.2 = (f32[17,3,33]{2,1,0:T(4,128)S(1)}, f32[17,3,33]{2,1,0:T(4,128)S(1)}, u32[]{:S(2)}, u32[]{:S(2)}) collective-permute-start(f32[17,3,33]{2,1,0:T(4,128)S(1)} %maximum_bitcast_fusion), channel_id=1, source_target_pairs={{1,0},{2,1},{3,2},{5,4},{6,5},{7,6},{9,8},{10,9},{11,10},{13,12},{... | collective-permute-start | bytes 20204 | tf_op jit(solution)/shard_map/ppermute | solution.py:21
  22.0 12.4 %energy.1 = (f32[16,32,256]{2,1,0:T(8,128)}, f32[32,128]{1,0:T(8,128)}) custom-call(s32[3]{0:T(128)} %pad_add_fusion.where_ref, f32[3,16,32,256]{3,2,1,0:T(8,128)} %u_ref.1, f32[3,1,32,256]{3,2,1,0:T(8,128)} %copy.53.xh_ref, f32[3,17,256]{2,1,0:T(8,128)} %copy.54.yh_ref, f32[17,8,128]{2,1,0:T(8,128)} %select_maximum_fusion.1.zh_ref, f32[16,32,256]{2,1,0:T(8,128)} %rho_ref.1, ...), custom_call_target="tpu_custom_call" | custom-call | tf_op jit(solution)/shard_map/energy/pallas_call | solution.py:193
  35.4 1.6 %copy.55 = f32[16,32,256]{1,2,0:T(8,128)S(1)} copy(f32[16,32,256]{2,1,0:T(8,128)} %get-tuple-element.5.w_ref) | data formatting | bytes 1048576 | tf_op jit(solution)/shard_map/energy/pallas_call | solution.py:193
  37.0 3.0 %all-to-all-start = ((f32[32,1,128]{2,1,0:T(1,128)}), f32[32,1,128]{2,1,0:T(1,128)S(1)}, u32[]{:S(2)}, u32[]{:S(2)}) async-start(f32[32,1,128]{2,1,0:T(1,128)} %bitcast.11), calls=%async_computation | async-start | bytes 32768 | tf_op jit(solution)/shard_map/all_to_all | solution.py:209
  40.1 1.3 %collective-permute-start.4 = (f32[2,32,256]{1,2,0:T(8,128)S(1)}, f32[2,32,256]{1,2,0:T(8,128)S(1)}, u32[]{:S(2)}, u32[]{:S(2)}) collective-permute-start(f32[2,32,256]{1,2,0:T(8,128)S(1)} %get-tuple-element.15), channel_id=1, source_target_pairs={{8,0},{16,8},{24,16},{9,1},{17,9},{25,17},{10,2},{18,10},{26,18},{... | collective-permute-start | bytes 196616 | tf_op jit(solution)/shard_map/ppermute | solution.py:21
  41.4 2.0 %copy.58 = f32[16,2,256]{1,2,0:T(8,128)} copy(f32[16,2,256]{2,1,0:T(2,128)S(1)} %get-tuple-element.17) | data formatting | bytes 65536 | tf_op jit(solution)/shard_map/slice | solution.py:213
  43.4 4.0 %collective-permute-start.3 = (f32[2,32,256]{1,2,0:T(8,128)S(1)}, f32[2,32,256]{1,2,0:T(8,128)S(1)}, u32[]{:S(2)}, u32[]{:S(2)}) collective-permute-start(f32[2,32,256]{1,2,0:T(8,128)S(1)} %get-tuple-element.16), channel_id=1, source_target_pairs={{0,8},{8,16},{16,24},{1,9},{9,17},{17,25},{2,10},{10,18},{18,26},{... | collective-permute-start | bytes 196616 | tf_op jit(solution)/shard_map/ppermute | solution.py:21
  47.4 2.0 %copy.57 = f32[16,2,256]{1,2,0:T(8,128)} copy(f32[16,2,256]{2,1,0:T(2,128)S(1)} %get-tuple-element.18) | data formatting | bytes 65536 | tf_op jit(solution)/shard_map/slice | solution.py:214
  49.9 2.6 %collective-permute-done.3 = f32[2,32,256]{1,2,0:T(8,128)S(1)} collective-permute-done((f32[2,32,256]{1,2,0:T(8,128)S(1)}, f32[2,32,256]{1,2,0:T(8,128)S(1)}, u32[]{:S(2)}, u32[]{:S(2)}) %collective-permute-start.3) | collective-permute-done | bytes 65568 | tf_op jit(solution)/shard_map/ppermute | solution.py:21
  52.6 2.0 %maximum_select_fusion = f32[20,2,256]{1,2,0:T(8,128)S(1)} fusion(f32[2,2,256]{1,2,0:T(8,128)S(1)} %get-tuple-element.26, f32[16,2,256]{1,2,0:T(8,128)} %copy.57, f32[2,2,256]{1,2,0:T(8,128)S(1)} %get-tuple-element.24, f32[2,2,256]{1,2,0:T(8,128)S(1)} %get-tuple-element.25, f32[16,2,256]{1,2,0:T(8,128)S(1)} %copy-done.1, ...), kind=kLoop, calls=%fused_computation | loop fusion | flops 51200 | bytes 122881 | tf_op jit(solution)/shard_map/jit(_where)/select_n | solution.py:28
  55.4 1.3 %collective-permute-start.5 = (f32[20,2,256]{2,1,0:T(2,128)S(1)}, f32[20,2,256]{2,1,0:T(2,128)S(1)}, u32[]{:S(2)}, u32[]{:S(2)}) collective-permute-start(f32[20,2,256]{2,1,0:T(2,128)S(1)} %copy.59), channel_id=1, source_target_pairs={{0,4},{4,0},{1,5},{5,1},{2,6},{6,2},{3,7},{7,3},{8,12},{12,8},{9,1... | collective-permute-start | bytes 122888 | tf_op jit(solution)/shard_map/ppermute | solution.py:28
  56.6 1.6 %collective-permute-done.5 = f32[20,2,256]{2,1,0:T(2,128)S(1)} collective-permute-done((f32[20,2,256]{2,1,0:T(2,128)S(1)}, f32[20,2,256]{2,1,0:T(2,128)S(1)}, u32[]{:S(2)}, u32[]{:S(2)}) %collective-permute-start.5) | collective-permute-done | bytes 40992 | tf_op jit(solution)/shard_map/ppermute | solution.py:28
  58.3 2.3 %copy.60 = f32[20,2,256]{1,2,0:T(8,128)} copy(f32[20,2,256]{2,1,0:T(2,128)S(1)} %collective-permute-done.5) | data formatting | bytes 81920 | tf_op jit(solution)/shard_map/ppermute | solution.py:28
  60.6 2.2 %broadcast_select_fusion = (f32[20,2,256]{1,2,0:T(8,128)S(1)}, f32[20,2,256]{1,2,0:T(8,128)S(1)}) fusion(f32[20,2,256]{1,2,0:T(8,128)} %copy.60, pred[]{:T(512)S(6)} %eq.8, pred[]{:T(512)S(6)} %eq.7), kind=kLoop, calls=%fused_computation.1 | loop fusion | flops 20480 | bytes 122882 | tf_op jit(solution)/shard_map/jit(_where)/select_n | solution.py:30
  62.8 1.5 %copy-done = f32[20,2,256]{1,2,0:T(8,128)} copy-done((f32[20,2,256]{1,2,0:T(8,128)}, f32[20,2,256]{1,2,0:T(8,128)S(1)}, u32[]{:S(2)}) %copy-start) | copy-done | bytes 40984
  64.5 4.5 %collective-permute-start.6 = (f32[20,2,40]{2,1,0:T(2,128)S(1)}, f32[20,2,40]{2,1,0:T(2,128)S(1)}, u32[]{:S(2)}, u32[]{:S(2)}) collective-permute-start(f32[20,2,40]{2,1,0:T(2,128)S(1)} %get-tuple-element.31), channel_id=1, source_target_pairs={{1,0},{2,1},{3,2},{5,4},{6,5},{7,6},{9,8},{10,9},{11,10},{13,12},{... | collective-permute-start | bytes 19208 | tf_op jit(solution)/shard_map/ppermute | solution.py:21
  68.9 3.2 %collective-permute-start.7 = (f32[20,2,40]{2,1,0:T(2,128)S(1)}, f32[20,2,40]{2,1,0:T(2,128)S(1)}, u32[]{:S(2)}, u32[]{:S(2)}) collective-permute-start(f32[20,2,40]{2,1,0:T(2,128)S(1)} %get-tuple-element.32), channel_id=1, source_target_pairs={{0,1},{1,2},{2,3},{4,5},{5,6},{6,7},{8,9},{9,10},{10,11},{12,13},{... | collective-permute-start | bytes 19208 | tf_op jit(solution)/shard_map/ppermute | solution.py:21
  75.5 3.1 %copy.67.yhi_ref = f32[20,2,256]{2,1,0:T(2,128)} copy(f32[20,2,256]{1,2,0:T(8,128)} %copy-done) | data formatting | bytes 81920 | tf_op jit(solution)/shard_map/jit(_where)/select_n | solution.py:30
  78.6 1.4 %copy.66.ylo_ref = f32[20,2,256]{2,1,0:T(2,128)} copy(f32[20,2,256]{1,2,0:T(8,128)S(1)} %get-tuple-element.12) | data formatting | bytes 81920 | tf_op jit(solution)/shard_map/jit(_where)/select_n | solution.py:30
  80.6 6.7 %cone.1 = f32[16,32,256]{2,1,0:T(8,128)} custom-call(f32[16,32,256]{2,1,0:T(8,128)} %get-tuple-element.5.w_ref, f32[2,32,256]{2,1,0:T(8,128)} %copy.64.xlo_ref, f32[2,32,256]{2,1,0:T(8,128)} %copy.65.xhi_ref, f32[20,2,256]{2,1,0:T(2,128)} %copy.66.ylo_ref, f32[20,2,256]{2,1,0:T(2,128)} %copy.67.yhi_ref, f32[20,8,128]{2,1,0:T(8,128)} %select_maximum_fusion.z_ref), custom_call_target="tpu_custom_call" | custom-call | tf_op jit(solution)/shard_map/cone/pallas_call | solution.py:226
  (44 shorter events, 11.7 us)
Async XLA Ops:
  0.6 9.6 %slice-start = ((f32[3,16,32,256]{3,2,1,0:T(8,128)}), f32[3,16,32,1]{3,2,1,0:T(8,128)S(1)}, s32[]{:S(2)}) async-start(f32[3,16,32,256]{3,2,1,0:T(8,128)} %u_ref.1), calls=%async_computation.1 | async-start | bytes 1572864 | tf_op jit(solution)/shard_map/slice | solution.py:181
  1.7 7.2 %collective-permute-start = (f32[3,1,32,256]{3,0,2,1:T(4,128)S(1)}, f32[3,1,32,256]{3,0,2,1:T(4,128)S(1)}, u32[]{:S(2)}, u32[]{:S(2)}) collective-permute-start(f32[3,1,32,256]{3,0,2,1:T(4,128)S(1)} %copy.69), channel_id=1, source_target_pairs={{8,0},{16,8},{24,16},{9,1},{17,9},{25,17},{10,2},{18,10},{26,18},{... | collective-permute-start | bytes 294920 | tf_op jit(solution)/shard_map/ppermute | solution.py:21
  8.9 5.1 %collective-permute-start.1 = (f32[3,17,256]{2,0,1:T(4,128)S(1)}, f32[3,17,256]{2,0,1:T(4,128)S(1)}, u32[]{:S(2)}, u32[]{:S(2)}) collective-permute-start(f32[3,17,256]{2,0,1:T(4,128)S(1)} %pad_maximum_fusion), channel_id=1, source_target_pairs={{4,0},{5,1},{6,2},{7,3},{12,8},{13,9},{14,10},{15,11},{20,16},{21,... | collective-permute-start | bytes 156680 | tf_op jit(solution)/shard_map/ppermute | solution.py:21
  14.1 7.2 %collective-permute-start.2 = (f32[17,3,33]{2,1,0:T(4,128)S(1)}, f32[17,3,33]{2,1,0:T(4,128)S(1)}, u32[]{:S(2)}, u32[]{:S(2)}) collective-permute-start(f32[17,3,33]{2,1,0:T(4,128)S(1)} %maximum_bitcast_fusion), channel_id=1, source_target_pairs={{1,0},{2,1},{3,2},{5,4},{6,5},{7,6},{9,8},{10,9},{11,10},{13,12},{... | collective-permute-start | bytes 20204 | tf_op jit(solution)/shard_map/ppermute | solution.py:21
  37.0 12.4 %all-to-all-start = ((f32[32,1,128]{2,1,0:T(1,128)}), f32[32,1,128]{2,1,0:T(1,128)S(1)}, u32[]{:S(2)}, u32[]{:S(2)}) async-start(f32[32,1,128]{2,1,0:T(1,128)} %bitcast.11), calls=%async_computation | async-start | bytes 32768 | tf_op jit(solution)/shard_map/all_to_all | solution.py:209
  40.1 9.6 %collective-permute-start.4 = (f32[2,32,256]{1,2,0:T(8,128)S(1)}, f32[2,32,256]{1,2,0:T(8,128)S(1)}, u32[]{:S(2)}, u32[]{:S(2)}) collective-permute-start(f32[2,32,256]{1,2,0:T(8,128)S(1)} %get-tuple-element.15), channel_id=1, source_target_pairs={{8,0},{16,8},{24,16},{9,1},{17,9},{25,17},{10,2},{18,10},{26,18},{... | collective-permute-start | bytes 196616 | tf_op jit(solution)/shard_map/ppermute | solution.py:21
  43.4 9.1 %collective-permute-start.3 = (f32[2,32,256]{1,2,0:T(8,128)S(1)}, f32[2,32,256]{1,2,0:T(8,128)S(1)}, u32[]{:S(2)}, u32[]{:S(2)}) collective-permute-start(f32[2,32,256]{1,2,0:T(8,128)S(1)} %get-tuple-element.16), channel_id=1, source_target_pairs={{0,8},{8,16},{16,24},{1,9},{9,17},{17,25},{2,10},{10,18},{18,26},{... | collective-permute-start | bytes 196616 | tf_op jit(solution)/shard_map/ppermute | solution.py:21
  49.5 3.2 %copy-start.1 = (f32[16,2,256]{1,2,0:T(8,128)S(1)}, f32[16,2,256]{1,2,0:T(8,128)}, u32[]{:S(2)}) copy-start(f32[16,2,256]{1,2,0:T(8,128)} %copy.58) | copy-start | bytes 98308
  55.4 2.9 %collective-permute-start.5 = (f32[20,2,256]{2,1,0:T(2,128)S(1)}, f32[20,2,256]{2,1,0:T(2,128)S(1)}, u32[]{:S(2)}, u32[]{:S(2)}) collective-permute-start(f32[20,2,256]{2,1,0:T(2,128)S(1)} %copy.59), channel_id=1, source_target_pairs={{0,4},{4,0},{1,5},{5,1},{2,6},{6,2},{3,7},{7,3},{8,12},{12,8},{9,1... | collective-permute-start | bytes 122888 | tf_op jit(solution)/shard_map/ppermute | solution.py:28
  62.8 1.5 %copy-start = (f32[20,2,256]{1,2,0:T(8,128)}, f32[20,2,256]{1,2,0:T(8,128)S(1)}, u32[]{:S(2)}) copy-start(f32[20,2,256]{1,2,0:T(8,128)S(1)} %get-tuple-element.11) | copy-start | bytes 122884
  64.5 15.5 %collective-permute-start.6 = (f32[20,2,40]{2,1,0:T(2,128)S(1)}, f32[20,2,40]{2,1,0:T(2,128)S(1)}, u32[]{:S(2)}, u32[]{:S(2)}) collective-permute-start(f32[20,2,40]{2,1,0:T(2,128)S(1)} %get-tuple-element.31), channel_id=1, source_target_pairs={{1,0},{2,1},{3,2},{5,4},{6,5},{7,6},{9,8},{10,9},{11,10},{13,12},{... | collective-permute-start | bytes 19208 | tf_op jit(solution)/shard_map/ppermute | solution.py:21
  68.9 11.0 %collective-permute-start.7 = (f32[20,2,40]{2,1,0:T(2,128)S(1)}, f32[20,2,40]{2,1,0:T(2,128)S(1)}, u32[]{:S(2)}, u32[]{:S(2)}) collective-permute-start(f32[20,2,40]{2,1,0:T(2,128)S(1)} %get-tuple-element.32), channel_id=1, source_target_pairs={{0,1},{1,2},{2,3},{4,5},{5,6},{6,7},{8,9},{9,10},{10,11},{12,13},{... | collective-permute-start | bytes 19208 | tf_op jit(solution)/shard_map/ppermute | solution.py:21

commit v2 on v1

--- a/solution.py
+++ b/solution.py
@@ -19,16 +19,6 @@
     count = lax.axis_size(axis)
     route = [(i + distance, i) for i in range(count) if 0 <= i + distance < count]
     return lax.ppermute(block, axis, route)
-
-
-def both_sides(low_part, high_part, axis):
-    count = lax.axis_size(axis)
-    if count == 2:
-        at = lax.axis_index(axis)
-        got = lax.ppermute(jnp.where(at == 0, high_part, low_part), axis, [(0, 1), (1, 0)])
-        zero = jnp.zeros_like(got)
-        return jnp.where(at == 1, got, zero), jnp.where(at == 0, got, zero)
-    return shift_from(high_part, axis, -1), shift_from(low_part, axis, 1)
 
 
 def missing(position, extent):
@@ -42,8 +32,8 @@
 
 
 def energy_kernel(
-    where_ref, u_ref, xh_ref, yh_ref, zh_ref, rho_ref, k_ref, w_ref, sums_ref, corners, gains, inv_ref,
-    *, extents
+    where_ref, u_ref, xh_ref, yh_ref, zh_ref, rho_ref, k_ref,
+    w_ref, low_ref, high_ref, sums_ref, corners, gains, inv_ref, *, extents
 ):
     planes, height, length = rho_ref.shape
     side = 24 * ROWS
@@ -121,47 +111,79 @@
     slot = (planes - 1) % 2
     prepare(lambda m: xh_ref[m, 0], planes, 1 - slot)
     total, amount = element_plane(planes - 1, slot, 1 - slot, sums)
-    at = lax.broadcasted_iota(jnp.int32, sums_ref.shape, 1)
+    low_ref[...] = w_ref[0:2]
+    high_ref[...] = w_ref[planes - 2 : planes]
+    at = lax.broadcasted_iota(jnp.int32, sums_ref.shape, 2)
     sums_ref[...] = jnp.where(at == 0, jnp.sum(total), jnp.where(at == 1, jnp.sum(amount), 0.0))
 
 
-def filter_kernel(w_ref, xlo_ref, xhi_ref, ylo_ref, yhi_ref, z_ref, out_ref, field):
-    planes, height, length = w_ref.shape
-    full_rows, full_lanes = field.shape[1:]
-
-    def fill(p, body):
-        field[p, 0:height, 0:length] = body
-        tail = jnp.concatenate(
-            [yhi_ref[p], jnp.zeros((ROWS - 4, length), F32), ylo_ref[p]], axis=0
-        )
-        field[p, height : height + ROWS, 0:length] = tail
-        z = z_ref[p]
-        block = jnp.concatenate([z[0:2], jnp.zeros((LANES - 4, LANES), F32), z[2:4]], axis=0)
-        field[p, :, length : length + LANES] = block.T[0:full_rows]
-
-    def box(v, axis):
-        n = v.shape[axis]
-        return v + pltpu.roll(v, 1, axis) + pltpu.roll(v, n - 1, axis)
-
-    for p in range(2):
-        fill(p, xlo_ref[p])
-        fill(planes + 2 + p, xhi_ref[p])
-
-    def middle(p, carry):
-        fill(p + 2, w_ref[p])
+def box(v, axis):
+    n = v.shape[axis]
+    return v + pltpu.roll(v, 1, axis) + pltpu.roll(v, n - 1, axis)
+
+
+def first_kernel(where_ref, w_ref, xlo_ref, xhi_ref, out_ref, *messages):
+    planes, height, _ = w_ref.shape
+
+    def emit(i, five):
+        a, b, c, d, e = five
+        t = (a + e) + 2.0 * (b + d) + 3.0 * c
+        out_ref[i] = t
+        low, high = t[0:2], t[height - 2 : height]
+        if len(messages) == 1:
+            messages[0][i] = jnp.where(where_ref[1] == 0, high, low)
+        else:
+            messages[0][i] = low
+            messages[1][i] = high
+
+    def plane(k):
+        if k < 0:
+            return xlo_ref[2 + k]
+        return w_ref[k] if k < planes else xhi_ref[k - planes]
+
+    for i in (0, 1, planes - 2, planes - 1):
+        emit(i, [plane(i + d) for d in range(-2, 3)])
+
+    def inner(i, carry):
+        emit(i, [w_ref[i + d] for d in range(-2, 3)])
         return carry
 
-    lax.fori_loop(0, planes, middle, 0)
+    lax.fori_loop(2, planes - 2, inner, 0, unroll=2)
+
+
+def second_kernel(where_ref, s_ref, *refs):
+    planes, height, length = s_ref.shape
+    messages, (out_ref, low_ref, high_ref) = refs[:-3], refs[-3:]
 
     def one(i, carry):
-        a, b, c, d, e = (field[i + k] for k in range(5))
-        t = (a + e) + 2.0 * (b + d) + 3.0 * c
+        if len(messages) == 1:
+            got = messages[0][i]
+            before = jnp.where(where_ref[1] == 1, got, 0.0)
+            after = jnp.where(where_ref[1] == 0, got, 0.0)
+        else:
+            before, after = messages[0][i], messages[1][i]
+        gap = jnp.zeros((ROWS - 4, length), F32)
+        t = jnp.concatenate([s_ref[i], after, gap, before], axis=0)
         t = box(box(t, 0), 0)[0:height]
-        t = box(box(t, 1), 1)
-        out_ref[i] = t[:, 0:length]
+        out_ref[i] = t
+        low_ref[i] = t[:, 0:LANES].T[0:2]
+        high_ref[i] = t[:, length - LANES : length].T[LANES - 2 : LANES]
         return carry
 
-    lax.fori_loop(0, planes, one, 0)
+    lax.fori_loop(0, planes, one, 0, unroll=2)
+
+
+def third_kernel(s_ref, zlo_ref, zhi_ref, out_ref):
+    planes, height, length = s_ref.shape
+
+    def one(i, carry):
+        gap = jnp.zeros((LANES - 4, height), F32)
+        side = jnp.concatenate([zhi_ref[i], gap, zlo_ref[i]], axis=0).T
+        t = jnp.concatenate([s_ref[i], side], axis=1)
+        out_ref[i] = box(box(t, 1), 1)[:, 0:length]
+        return carry
+
+    lax.fori_loop(0, planes, one, 0, unroll=2)
 
 
 VMEM = pl.BlockSpec(memory_space=pltpu.VMEM)
@@ -190,13 +212,18 @@
         axis=1,
     )
 
-    weighted, sums = pl.pallas_call(
+    def shape(*dims):
+        return jax.ShapeDtypeStruct(dims, F32)
+
+    weighted, low, high, sums = pl.pallas_call(
         functools.partial(energy_kernel, extents=extents),
         in_specs=[SMEM] + [VMEM] * 6,
-        out_specs=[VMEM, VMEM],
+        out_specs=[VMEM] * 4,
         out_shape=[
-            jax.ShapeDtypeStruct(density.shape, F32),
-            jax.ShapeDtypeStruct((devices, LANES), F32),
+            shape(planes, height, length),
+            shape(2, height, length),
+            shape(2, height, length),
+            shape(devices, 1, LANES),
         ],
         scratch_shapes=[
             pltpu.VMEM((2, 12, height, length), F32),
@@ -206,31 +233,39 @@
         name="energy",
     )(where, displacement, xh, yh, zh, density, stiffness)
 
+    xlo = shift_from(high, "gx", -1)
+    xhi = shift_from(low, "gx", 1)
     gathered = lax.all_to_all(sums, AXES, 0, 0, tiled=True)
-    totals = jnp.sum(gathered, axis=0)
-
-    xlo, xhi = both_sides(weighted[:2], weighted[-2:], "gx")
-    low = jnp.concatenate([v[:, :2] for v in (xlo, weighted, xhi)], axis=0)
-    high = jnp.concatenate([v[:, -2:] for v in (xlo, weighted, xhi)], axis=0)
-    ylo, yhi = both_sides(low, high, "gy")
-
-    def columns(part):
-        middle = jnp.concatenate([v[..., part] for v in (xlo, weighted, xhi)], axis=0)
-        gap = jnp.zeros((planes + 4, ROWS - 4, 2), F32)
-        whole = jnp.concatenate([middle, yhi[..., part], gap, ylo[..., part]], axis=1)
-        return whole.transpose(0, 2, 1)
-
-    zlo, zhi = both_sides(columns(slice(0, 2)), columns(slice(length - 2, length)), "gz")
-    z = jnp.pad(jnp.concatenate([zhi, zlo], axis=1), ((0, 0), (0, 4), (0, LANES - height - ROWS)))
-
+    totals = jnp.sum(gathered, axis=(0, 1))
+
+    rows = 1 if sizes[1] == 2 else 2
+    smooth, *parts = pl.pallas_call(
+        first_kernel,
+        in_specs=[SMEM] + [VMEM] * 3,
+        out_specs=[VMEM] * (1 + rows),
+        out_shape=[shape(planes, height, length)] + [shape(planes, 2, length)] * rows,
+        name="along_x",
+    )(where, weighted, xlo, xhi)
+    if rows == 1:
+        parts = [lax.ppermute(parts[0], "gy", [(0, 1), (1, 0)])]
+    else:
+        parts = [shift_from(parts[1], "gy", -1), shift_from(parts[0], "gy", 1)]
+    smooth, low, high = pl.pallas_call(
+        second_kernel,
+        in_specs=[SMEM] + [VMEM] * (1 + rows),
+        out_specs=[VMEM] * 3,
+        out_shape=[shape(planes, height, length)] + [shape(planes, 2, height)] * 2,
+        name="along_y",
+    )(where, smooth, *parts)
+    zlo = shift_from(high, "gz", -1)
+    zhi = shift_from(low, "gz", 1)
     filtered = pl.pallas_call(
-        filter_kernel,
-        in_specs=[VMEM] * 6,
+        third_kernel,
+        in_specs=[VMEM] * 3,
         out_specs=VMEM,
-        out_shape=jax.ShapeDtypeStruct(density.shape, F32),
-        scratch_shapes=[pltpu.VMEM((planes + 4, height + ROWS, length + LANES), F32)],
-        name="cone",
-    )(weighted, xlo, xhi, ylo, yhi, z)
+        out_shape=shape(planes, height, length),
+        name="along_z",
+    )(smooth, zlo, zhi)
 
     cells = float(extents[0] * extents[1] * extents[2])
     return filtered, totals[0] / cells, totals[1] / cells

time: 90.3 us -> 76.3 us (0.84)
  local copies, waits for them, and re-layouts: 22.2 us -> 6.48 us
  blocking collectives: 0 us -> 11.5 us
  starting transfers between devices: 24.1 us -> 16 us
  other arithmetic: 6.41 us -> 1.43 us
  Pallas kernels: 19.1 us -> 21.8 us
  waiting for transfers between devices: 13.4 us -> 14.4 us
    all_to_all x0 -> x1, blocking collectives: none -> 11.5 us  [on_device(): gathered = lax.all_to_all(sums, AXES, 0, 0, tiled=True)]
    slice x10 -> x0, local copies, waits for them, and re-layouts: 5.3 us -> none  [the longest x4 3.21 us: on_device(): low = jnp.concatenate([v[:, :2] for v in (xlo, weighted, xhi)], axis=0)]
    select_n x3 -> x0, local copies, waits for them, and re-layouts: 5.26 us -> none  [the longest x2 4.5 us: both_sides(): return (jnp.where(at == 1, got, zero), jnp.where(at == 0, got, zero))]
    select_n x2 -> x0, other arithmetic: 4.16 us -> none  [the longest x1 2.19 us: both_sides(): return (jnp.where(at == 1, got, zero), jnp.where(at == 0, got, zero))]
    ppermute x7, starting transfers between devices: 19.8 us -> 16 us  [shift_from(): return lax.ppermute(block, axis, route)]
    all_to_all x1 -> x0, starting transfers between devices: 3.03 us -> none  [on_device(): gathered = lax.all_to_all(sums, AXES, 0, 0, tiled=True)]
    pallas_call x1 -> x3, Pallas kernels: 6.68 us -> 9.36 us  [the longest x1 4.55 us: on_device(): pl.pallas_call(third_kernel, in_specs=[VMEM] * 3, out_specs=VMEM, out_sha...]
    ppermute x7, waiting for transfers between devices: 11.8 us -> 14.4 us  [shift_from(): return lax.ppermute(block, axis, route)]
  transfers between devices with their start and end apart: 9 -> 8, of which waited for: 6 -> 6; matrix products, arithmetic and copies ran while one was open for 16% -> 6% of each run, Pallas kernels for 0% -> 0%
where the time goes in v2:
time: 76.3 us; the launch traced here: 75.8 us
  Pallas kernels  21.8 us (29%)
  starting transfers between devices  16 us (21%)
  waiting for transfers between devices  14.4 us (19%)
  blocking collectives  11.5 us (15%)
  local copies, waits for them, and re-layouts  6.48 us (8%)
  between operations  4.34 us (6%)
  other arithmetic  1.43 us (2%)
    ppermute x7, starting transfers between devices, shift_from(): return lax.ppermute(block, axis, route)  16 us
    ppermute x7, waiting for transfers between devices, shift_from(): return lax.ppermute(block, axis, route)  14.4 us
    pallas_call x1, Pallas kernels, on_device(): pl.pallas_call(functools.partial(energy_kernel, extents=extents), in_spec...  12.4 us
    all_to_all x1, blocking collectives, on_device(): gathered = lax.all_to_all(sums, AXES, 0, 0, tiled=True)  11.5 us
    pallas_call x1, Pallas kernels, on_device(): pl.pallas_call(third_kernel, in_specs=[VMEM] * 3, out_specs=VMEM, out_sha...  4.55 us
    pallas_call x1, Pallas kernels, on_device(): pl.pallas_call(second_kernel, in_specs=[SMEM] + [VMEM] * (1 + rows), out_...  2.74 us
    unnamed x13, local copies, waits for them, and re-layouts  2.38 us
    pallas_call x1, Pallas kernels, on_device(): pl.pallas_call(first_kernel, in_specs=[SMEM] + [VMEM] * 3, out_specs=[VME...  2.07 us
  transfers between devices with their start and end apart: 8, of which 6 were waited for; matrix products, arithmetic and copies ran while one was open for 6% of the time, Pallas kernels for 0%

profile of v2, /device:TPU:1, one launch (start us, length us, event | category | flops | bytes accessed | tf_op | source)
XLA Modules:
  0.0 75.8 jit_solution(13751718326113824799)
XLA Ops:
  0.6 1.0 %slice.30 = f32[3,1,32,256]{3,2,1,0:T(8,128)S(1)} slice(f32[3,16,32,256]{3,2,1,0:T(8,128)} %u_ref.1), slice={[0:3], [0:1], [0:32], [0:256]} | slice | bytes 196608 | tf_op jit(solution)/shard_map/slice | solution.py:200
  1.7 1.3 %collective-permute-start = (f32[3,1,32,256]{3,0,2,1:T(4,128)S(1)}, f32[3,1,32,256]{3,0,2,1:T(4,128)S(1)}, u32[]{:S(2)}, u32[]{:S(2)}) collective-permute-start(f32[3,1,32,256]{3,0,2,1:T(4,128)S(1)} %copy.13), channel_id=1, source_target_pairs={{8,0},{16,8},{24,16},{9,1},{17,9},{25,17},{10,2},{18,10},{26,18},{... | collective-permute-start | bytes 294920 | tf_op jit(solution)/shard_map/ppermute | solution.py:21
  3.0 1.0 %slice.31 = f32[3,16,1,256]{3,2,1,0:T(1,128)S(1)} slice(f32[3,16,32,256]{3,2,1,0:T(8,128)} %u_ref.1), slice={[0:3], [0:16], [0:1], [0:256]} | slice | bytes 98304 | tf_op jit(solution)/shard_map/slice | solution.py:201
  4.1 4.8 %collective-permute-done = f32[3,1,32,256]{3,0,2,1:T(4,128)S(1)} collective-permute-done((f32[3,1,32,256]{3,0,2,1:T(4,128)S(1)}, f32[3,1,32,256]{3,0,2,1:T(4,128)S(1)}, u32[]{:S(2)}, u32[]{:S(2)}) %collective-permute-start) | collective-permute-done | bytes 98336 | tf_op jit(solution)/shard_map/ppermute | solution.py:21
  8.9 1.3 %collective-permute-start.1 = (f32[3,17,256]{2,0,1:T(4,128)S(1)}, f32[3,17,256]{2,0,1:T(4,128)S(1)}, u32[]{:S(2)}, u32[]{:S(2)}) collective-permute-start(f32[3,17,256]{2,0,1:T(4,128)S(1)} %pad_maximum_fusion), channel_id=1, source_target_pairs={{4,0},{5,1},{6,2},{7,3},{12,8},{13,9},{14,10},{15,11},{20,16},{21,... | collective-permute-start | bytes 156680 | tf_op jit(solution)/shard_map/ppermute | solution.py:21
  10.8 3.2 %collective-permute-done.1 = f32[3,17,256]{2,0,1:T(4,128)S(1)} collective-permute-done((f32[3,17,256]{2,0,1:T(4,128)S(1)}, f32[3,17,256]{2,0,1:T(4,128)S(1)}, u32[]{:S(2)}, u32[]{:S(2)}) %collective-permute-start.1) | collective-permute-done | bytes 52256 | tf_op jit(solution)/shard_map/ppermute | solution.py:21
  14.1 4.3 %collective-permute-start.2 = (f32[17,3,33]{2,1,0:T(4,128)S(1)}, f32[17,3,33]{2,1,0:T(4,128)S(1)}, u32[]{:S(2)}, u32[]{:S(2)}) collective-permute-start(f32[17,3,33]{2,1,0:T(4,128)S(1)} %maximum_bitcast_fusion), channel_id=1, source_target_pairs={{1,0},{2,1},{3,2},{5,4},{6,5},{7,6},{9,8},{10,9},{11,10},{13,12},{... | collective-permute-start | bytes 20204 | tf_op jit(solution)/shard_map/ppermute | solution.py:21
  18.4 0.6 pad_add_fusion.where_ref
  19.0 0.7 copy.11.xh_ref
  19.7 0.6 copy.12.yh_ref
  20.3 0.9 %collective-permute-done.2 = f32[17,3,33]{2,1,0:T(4,128)S(1)} collective-permute-done((f32[17,3,33]{2,1,0:T(4,128)S(1)}, f32[17,3,33]{2,1,0:T(4,128)S(1)}, u32[]{:S(2)}, u32[]{:S(2)}) %collective-permute-start.2) | collective-permute-done | bytes 6764 | tf_op jit(solution)/shard_map/ppermute | solution.py:21
  21.3 0.7 select_maximum_fusion.zh_ref
  22.0 12.4 %energy.1 = (f32[16,32,256]{2,1,0:T(8,128)}, f32[2,32,256]{2,1,0:T(8,128)}, f32[2,32,256]{2,1,0:T(8,128)}, f32[32,1,128]{2,1,0:T(1,128)}) custom-call(s32[3]{0:T(128)} %pad_add_fusion.where_ref, f32[3,16,32,256]{3,2,1,0:T(8,128)} %u_ref.1, f32[3,1,32,256]{3,2,1,0:T(8,128)} %copy.11.xh_ref, f32[3,17,256]{2,1,0:T(8,128)} %copy.12.yh_ref, ...), custom_call_target="tpu_custom_call" | custom-call | tf_op jit(solution)/shard_map/energy/pallas_call | solution.py:218
  34.4 3.2 %collective-permute-start.3 = (f32[2,32,256]{2,1,0:T(8,128)}, f32[2,32,256]{2,1,0:T(8,128)S(1)}, u32[]{:S(2)}, u32[]{:S(2)}) collective-permute-start(f32[2,32,256]{2,1,0:T(8,128)} %get-tuple-element.13), channel_id=1, source_target_pairs={{0,8},{8,16},{16,24},{1,9},{9,17},{17,25},{2,10},{10,18},{18,26},{... | collective-permute-start | bytes 196616 | tf_op jit(solution)/shard_map/ppermute | solution.py:21
  37.6 1.3 %collective-permute-start.4 = (f32[2,32,256]{2,1,0:T(8,128)}, f32[2,32,256]{2,1,0:T(8,128)S(1)}, u32[]{:S(2)}, u32[]{:S(2)}) collective-permute-start(f32[2,32,256]{2,1,0:T(8,128)} %get-tuple-element.14), channel_id=1, source_target_pairs={{8,0},{16,8},{24,16},{9,1},{17,9},{25,17},{10,2},{18,10},{26,18},{... | collective-permute-start | bytes 196616 | tf_op jit(solution)/shard_map/ppermute | solution.py:21
  39.2 3.6 %collective-permute-done.4.xhi_ref = f32[2,32,256]{2,1,0:T(8,128)S(1)} collective-permute-done((f32[2,32,256]{2,1,0:T(8,128)}, f32[2,32,256]{2,1,0:T(8,128)S(1)}, u32[]{:S(2)}, u32[]{:S(2)}) %collective-permute-start.4) | collective-permute-done | bytes 65568 | tf_op jit(solution)/shard_map/ppermute | solution.py:21
  42.9 0.6 copy-done.1
  43.5 2.1 %along_x.1 = (f32[16,32,256]{2,1,0:T(8,128)}, f32[16,2,256]{2,1,0:T(2,128)}) custom-call(s32[3]{0:T(128)} %pad_add_fusion.where_ref, f32[16,32,256]{2,1,0:T(8,128)} %get-tuple-element.12.w_ref, f32[2,32,256]{2,1,0:T(8,128)} %copy-done, f32[2,32,256]{2,1,0:T(8,128)} %copy-done.1), custom_call_target="tpu_custom_call" | custom-call | tf_op jit(solution)/shard_map/along_x/pallas_call | solution.py:242
  45.6 11.5 %all_to_all.5 = f32[32,1,128]{2,1,0:T(1,128)S(1)} all-to-all(f32[32,1,128]{2,1,0:T(1,128)} %get-tuple-element.20), channel_id=1, replica_groups=mesh['gx'=4,'gy'=2,'gz'=4] {'gx','gy','gz'}, dimensions={0} | all-to-all | bytes 32768 | tf_op jit(solution)/shard_map/all_to_all | solution.py:238
  57.7 2.7 %along_y.1 = (f32[16,32,256]{2,1,0:T(8,128)}, f32[16,2,32]{2,1,0:T(2,128)}, f32[16,2,32]{2,1,0:T(2,128)}) custom-call(s32[3]{0:T(128)} %pad_add_fusion.where_ref, f32[16,32,256]{2,1,0:T(8,128)} %get-tuple-element.15.s_ref, f32[16,2,256]{2,1,0:T(2,128)} %copy-done.2), custom_call_target="tpu_custom_call" | custom-call | tf_op jit(solution)/shard_map/along_y/pallas_call | solution.py:253
  60.5 2.7 %collective-permute-start.6 = (f32[16,2,32]{2,1,0:T(2,128)}, f32[16,2,32]{2,1,0:T(2,128)S(1)}, u32[]{:S(2)}, u32[]{:S(2)}) collective-permute-start(f32[16,2,32]{2,1,0:T(2,128)} %get-tuple-element.18), channel_id=1, source_target_pairs={{0,1},{1,2},{2,3},{4,5},{5,6},{6,7},{8,9},{9,10},{10,11},{12,13},{... | collective-permute-start | bytes 12296 | tf_op jit(solution)/shard_map/ppermute | solution.py:21
  63.1 1.9 %collective-permute-start.7 = (f32[16,2,32]{2,1,0:T(2,128)}, f32[16,2,32]{2,1,0:T(2,128)S(1)}, u32[]{:S(2)}, u32[]{:S(2)}) collective-permute-start(f32[16,2,32]{2,1,0:T(2,128)} %get-tuple-element.19), channel_id=1, source_target_pairs={{1,0},{2,1},{3,2},{5,4},{6,5},{7,6},{9,8},{10,9},{11,10},{13,12},{... | collective-permute-start | bytes 12296 | tf_op jit(solution)/shard_map/ppermute | solution.py:21
  67.0 1.4 %collective-permute-done.7.zhi_ref = f32[16,2,32]{2,1,0:T(2,128)S(1)} collective-permute-done((f32[16,2,32]{2,1,0:T(2,128)}, f32[16,2,32]{2,1,0:T(2,128)S(1)}, u32[]{:S(2)}, u32[]{:S(2)}) %collective-permute-start.7) | collective-permute-done | bytes 4128 | tf_op jit(solution)/shard_map/ppermute | solution.py:21
  69.0 4.5 %along_z.1 = f32[16,32,256]{2,1,0:T(8,128)} custom-call(f32[16,32,256]{2,1,0:T(8,128)} %get-tuple-element.17.s_ref, f32[16,2,32]{2,1,0:T(2,128)} %copy-done.3, f32[16,2,32]{2,1,0:T(2,128)} %copy-done.4), custom_call_target="tpu_custom_call" | custom-call | tf_op jit(solution)/shard_map/along_z/pallas_call | solution.py:262
  (28 shorter events, 3.1 us)
Async XLA Ops:
  0.6 9.6 %slice-start = ((f32[3,16,32,256]{3,2,1,0:T(8,128)}), f32[3,16,32,1]{3,2,1,0:T(8,128)S(1)}, s32[]{:S(2)}) async-start(f32[3,16,32,256]{3,2,1,0:T(8,128)} %u_ref.1), calls=%async_computation.1 | async-start | bytes 1572864 | tf_op jit(solution)/shard_map/slice | solution.py:203
  1.7 7.2 %collective-permute-start = (f32[3,1,32,256]{3,0,2,1:T(4,128)S(1)}, f32[3,1,32,256]{3,0,2,1:T(4,128)S(1)}, u32[]{:S(2)}, u32[]{:S(2)}) collective-permute-start(f32[3,1,32,256]{3,0,2,1:T(4,128)S(1)} %copy.13), channel_id=1, source_target_pairs={{8,0},{16,8},{24,16},{9,1},{17,9},{25,17},{10,2},{18,10},{26,18},{... | collective-permute-start | bytes 294920 | tf_op jit(solution)/shard_map/ppermute | solution.py:21
  8.9 5.1 %collective-permute-start.1 = (f32[3,17,256]{2,0,1:T(4,128)S(1)}, f32[3,17,256]{2,0,1:T(4,128)S(1)}, u32[]{:S(2)}, u32[]{:S(2)}) collective-permute-start(f32[3,17,256]{2,0,1:T(4,128)S(1)} %pad_maximum_fusion), channel_id=1, source_target_pairs={{4,0},{5,1},{6,2},{7,3},{12,8},{13,9},{14,10},{15,11},{20,16},{21,... | collective-permute-start | bytes 156680 | tf_op jit(solution)/shard_map/ppermute | solution.py:21
  14.1 7.2 %collective-permute-start.2 = (f32[17,3,33]{2,1,0:T(4,128)S(1)}, f32[17,3,33]{2,1,0:T(4,128)S(1)}, u32[]{:S(2)}, u32[]{:S(2)}) collective-permute-start(f32[17,3,33]{2,1,0:T(4,128)S(1)} %maximum_bitcast_fusion), channel_id=1, source_target_pairs={{1,0},{2,1},{3,2},{5,4},{6,5},{7,6},{9,8},{10,9},{11,10},{13,12},{... | collective-permute-start | bytes 20204 | tf_op jit(solution)/shard_map/ppermute | solution.py:21
  34.4 4.8 %collective-permute-start.3 = (f32[2,32,256]{2,1,0:T(8,128)}, f32[2,32,256]{2,1,0:T(8,128)S(1)}, u32[]{:S(2)}, u32[]{:S(2)}) collective-permute-start(f32[2,32,256]{2,1,0:T(8,128)} %get-tuple-element.13), channel_id=1, source_target_pairs={{0,8},{8,16},{16,24},{1,9},{9,17},{17,25},{2,10},{10,18},{18,26},{... | collective-permute-start | bytes 196616 | tf_op jit(solution)/shard_map/ppermute | solution.py:21
  37.6 5.3 %collective-permute-start.4 = (f32[2,32,256]{2,1,0:T(8,128)}, f32[2,32,256]{2,1,0:T(8,128)S(1)}, u32[]{:S(2)}, u32[]{:S(2)}) collective-permute-start(f32[2,32,256]{2,1,0:T(8,128)} %get-tuple-element.14), channel_id=1, source_target_pairs={{8,0},{16,8},{24,16},{9,1},{17,9},{25,17},{10,2},{18,10},{26,18},{... | collective-permute-start | bytes 196616 | tf_op jit(solution)/shard_map/ppermute | solution.py:21
  39.2 3.6 %copy-start = (f32[2,32,256]{2,1,0:T(8,128)}, f32[2,32,256]{2,1,0:T(8,128)S(1)}, u32[]{:S(2)}) copy-start(f32[2,32,256]{2,1,0:T(8,128)S(1)} %collective-permute-done.3.xlo_ref) | copy-start | bytes 196612
  42.9 0.6 copy-start.1
  45.6 11.6 %collective-permute-start.5 = (f32[16,2,256]{2,1,0:T(2,128)}, f32[16,2,256]{2,1,0:T(2,128)S(1)}, u32[]{:S(2)}, u32[]{:S(2)}) collective-permute-start(f32[16,2,256]{2,1,0:T(2,128)} %get-tuple-element.16), channel_id=1, source_target_pairs={{0,4},{4,0},{1,5},{5,1},{2,6},{6,2},{3,7},{7,3},{8,12},{12,8},{9,1... | collective-permute-start | bytes 98312 | tf_op jit(solution)/shard_map/ppermute | solution.py:250
  57.1 0.6 copy-start.2
  60.5 6.5 %collective-permute-start.6 = (f32[16,2,32]{2,1,0:T(2,128)}, f32[16,2,32]{2,1,0:T(2,128)S(1)}, u32[]{:S(2)}, u32[]{:S(2)}) collective-permute-start(f32[16,2,32]{2,1,0:T(2,128)} %get-tuple-element.18), channel_id=1, source_target_pairs={{0,1},{1,2},{2,3},{4,5},{5,6},{6,7},{8,9},{9,10},{10,11},{12,13},{... | collective-permute-start | bytes 12296 | tf_op jit(solution)/shard_map/ppermute | solution.py:21
  63.1 5.3 %collective-permute-start.7 = (f32[16,2,32]{2,1,0:T(2,128)}, f32[16,2,32]{2,1,0:T(2,128)S(1)}, u32[]{:S(2)}, u32[]{:S(2)}) collective-permute-start(f32[16,2,32]{2,1,0:T(2,128)} %get-tuple-element.19), channel_id=1, source_target_pairs={{1,0},{2,1},{3,2},{5,4},{6,5},{7,6},{9,8},{10,9},{11,10},{13,12},{... | collective-permute-start | bytes 12296 | tf_op jit(solution)/shard_map/ppermute | solution.py:21
  67.0 1.4 %copy-start.3 = (f32[16,2,32]{2,1,0:T(2,128)}, f32[16,2,32]{2,1,0:T(2,128)S(1)}, u32[]{:S(2)}) copy-start(f32[16,2,32]{2,1,0:T(2,128)S(1)} %collective-permute-done.6.zlo_ref) | copy-start | bytes 12292
  68.4 0.6 copy-start.4

commit v3 on v2

v3 whole, which is shorter than its diff:
```python
import functools

import jax
import jax.numpy as jnp
from jax import lax
from jax.experimental import pallas as pl
from jax.experimental.pallas import tpu as pltpu
from jax.sharding import PartitionSpec as P


VOID = 0.001
AXES = ("gx", "gy", "gz")
F32 = jnp.float32
BF16 = jnp.bfloat16
LANES = 128
ROWS = 8


def shift_from(block, axis, distance):
    count = lax.axis_size(axis)
    route = [(i + distance, i) for i in range(count) if 0 <= i + distance < count]
    return lax.ppermute(block, axis, route)


def missing(position, extent):
    lost = (
        3.0 * (position == 0).astype(F32)
        + 1.0 * (position == 1).astype(F32)
        + 3.0 * (position == extent - 1).astype(F32)
        + 1.0 * (position == extent - 2).astype(F32)
    )
    return 9.0 - lost


def setup_kernel(where_ref, k_ref, gains, inv_ref, *, extents):
    height, length = inv_ref.shape
    side = 24 * ROWS
    k = k_ref[...]
    k_hi = k.astype(BF16)
    k_lo = (k - k_hi.astype(F32)).astype(BF16)
    r0 = lax.broadcasted_iota(jnp.int32, (side, 24), 0)
    r1 = lax.broadcasted_iota(jnp.int32, (side, 24), 1)
    spread = (r0 // ROWS == r1).astype(F32).astype(BF16)
    d0 = lax.broadcasted_iota(jnp.int32, (side, side), 0)
    d1 = lax.broadcasted_iota(jnp.int32, (side, side), 1)
    same_row = (d0 % ROWS) == (d1 % ROWS)
    for part, kk in enumerate((k_hi, k_lo)):
        tall = jnp.dot(spread, kk, preferred_element_type=F32).astype(BF16)
        full = lax.dot_general(tall, spread, (((1,), (1,)), ((), ())), preferred_element_type=F32)
        gains[part * side : (part + 1) * side, :] = jnp.where(same_row, full, 0.0).astype(BF16)

    row = lax.broadcasted_iota(jnp.int32, (height, length), 0)
    lane = lax.broadcasted_iota(jnp.int32, (height, length), 1)
    second = missing(row + where_ref[1] * height, extents[1])
    third = missing(lane + where_ref[2] * length, extents[2])
    inv_ref[...] = (-3.0 * (1.0 - VOID)) / (second * third)


def prepare(corners, slot, plane_of, row_of, columns):
    height, length = corners.shape[2:]
    last_row = lax.broadcasted_iota(jnp.int32, (height, length), 0) == height - 1
    last_lane = lax.broadcasted_iota(jnp.int32, (height, length), 1) == length - 1
    turned = jnp.concatenate([columns, jnp.zeros((ROWS - 3, LANES), F32)], axis=0).T
    for m in range(3):
        plane = plane_of(m)
        right = jnp.where(last_lane, turned[0:height, m : m + 1], pltpu.roll(plane, length - 1, 1))
        corners[slot, 4 * m + 0] = plane
        corners[slot, 4 * m + 1] = right
        corners[slot, 4 * m + 2] = jnp.where(last_row, row_of(m, 0), pltpu.roll(plane, height - 1, 0))
        corners[slot, 4 * m + 3] = jnp.where(last_row, row_of(m, 1), pltpu.roll(right, height - 1, 0))


def element_plane(corners, slots, gains, inv_ref, first, rho_of, store, sums):
    height, length = inv_ref.shape
    side = 24 * ROWS
    total, amount = sums
    inv_first = 1.0 / first
    for j in range(height // ROWS):
        rows = slice(j * ROWS, (j + 1) * ROWS)
        x = jnp.concatenate(
            [
                corners[slots[a], 4 * m + 2 * b + c, rows, :]
                for m in range(3)
                for a in range(2)
                for b in range(2)
                for c in range(2)
            ],
            axis=0,
        )
        h = x.astype(BF16)
        y = jnp.dot(gains[...], h, preferred_element_type=F32)
        y = y[:side] + y[side:]
        e = ((2.0 * x - h.astype(F32)) * y).reshape(24, ROWS, length).sum(axis=0)
        rho = rho_of(rows)
        square = rho * rho
        store(rows, square * e * (inv_ref[rows, :] * inv_first))
        total = total + (VOID + square * rho * (1.0 - VOID)) * e
        amount = amount + rho
    return total, amount


def main_kernel(
    where_ref, u_ref, yh_ref, zh_ref, rho_ref, gains, inv_ref, w_ref, low_ref, sums_ref, corners,
    *, extent
):
    planes, _, length = rho_ref.shape

    def load(p, slot):
        prepare(
            corners,
            slot,
            lambda m: u_ref[m, p],
            lambda m, c: yh_ref[m, pl.ds(p, 1), c : c + length],
            zh_ref[p],
        )

    load(0, 0)

    def one(i, slot, sums):
        load(i + 1, 1 - slot)
        at = where_ref[0] * planes + i + jnp.zeros((ROWS, length), jnp.int32)

        def store(rows, value):
            w_ref[i, rows, :] = value

        return element_plane(
            corners, (slot, 1 - slot), gains, inv_ref, missing(at, extent),
            lambda rows: rho_ref[i, rows, :], store, sums,
        )

    zero = jnp.zeros((ROWS, length), F32)
    pairs = (planes - 1) // 2
    sums = lax.fori_loop(0, pairs, lambda t, s: one(2 * t + 1, 1, one(2 * t, 0, s)), (zero, zero))
    for i in range(2 * pairs, planes - 1):
        sums = one(i, i % 2, sums)
    sums_ref[0], sums_ref[1] = sums
    low_ref[...] = w_ref[0:2]


def last_kernel(
    where_ref, u_ref, xh_ref, edge_ref, yh_ref, zh_ref, rho_ref, gains, inv_ref, w_ref, part_ref,
    high_ref, sums_ref, corners, *, extent, planes
):
    length = rho_ref.shape[2]
    last = planes - 1
    prepare(
        corners, 0, lambda m: u_ref[m, 0], lambda m, c: yh_ref[m, last : last + 1, c : c + length], zh_ref[last]
    )
    far = (length // LANES + 1) * LANES
    prepare(
        corners, 1, lambda m: xh_ref[m, 0], lambda m, c: edge_ref[m : m + 1, c : c + length],
        edge_ref[:, far : far + LANES],
    )
    at = where_ref[0] * planes + last + jnp.zeros((ROWS, length), jnp.int32)

    def store(rows, value):
        high_ref[1, rows, :] = value

    total, amount = element_plane(
        corners, (0, 1), gains, inv_ref, missing(at, extent), lambda rows: rho_ref[0, rows, :], store,
        (part_ref[0], part_ref[1]),
    )
    high_ref[0] = w_ref[0]
    at = lax.broadcasted_iota(jnp.int32, sums_ref.shape, 2)
    sums_ref[...] = jnp.where(at == 0, jnp.sum(total), jnp.where(at == 1, jnp.sum(amount), 0.0))


def box(v, axis):
    n = v.shape[axis]
    return v + pltpu.roll(v, 1, axis) + pltpu.roll(v, n - 1, axis)


def first_kernel(where_ref, w_ref, own_ref, xlo_ref, xhi_ref, out_ref, *messages):
    planes, height, _ = w_ref.shape

    def emit(i, five):
        a, b, c, d, e = five
        t = (a + e) + 2.0 * (b + d) + 3.0 * c
        out_ref[i] = t
        low, high = t[0:2], t[height - 2 : height]
        if len(messages) == 1:
            messages[0][i] = jnp.where(where_ref[1] == 0, high, low)
        else:
            messages[0][i] = low
            messages[1][i] = high

    def plane(k):
        if k < 0:
            return xlo_ref[2 + k]
        if k == planes - 1:
            return own_ref[1]
        return w_ref[k] if k < planes else xhi_ref[k - planes]

    for i in (0, 1, planes - 3, planes - 2, planes - 1):
        emit(i, [plane(i + d) for d in range(-2, 3)])

    def inner(i, carry):
        emit(i, [w_ref[i + d] for d in range(-2, 3)])
        return carry

    lax.fori_loop(2, planes - 3, inner, 0, unroll=True)


def second_kernel(where_ref, s_ref, *refs):
    planes, height, length = s_ref.shape
    messages, (out_ref, low_ref, high_ref) = refs[:-3], refs[-3:]

    def one(i, carry):
        if len(messages) == 1:
            got = messages[0][i]
            before = jnp.where(where_ref[1] == 1, got, 0.0)
            after = jnp.where(where_ref[1] == 0, got, 0.0)
        else:
            before, after = messages[0][i], messages[1][i]
        gap = jnp.zeros((ROWS - 4, length), F32)
        t = jnp.concatenate([s_ref[i], after, gap, before], axis=0)
        t = box(box(t, 0), 0)[0:height]
        out_ref[i] = t
        low_ref[i] = t[:, 0:LANES].T[0:2]
        high_ref[i] = t[:, length - LANES : length].T[LANES - 2 : LANES]
        return carry

    lax.fori_loop(0, planes, one, 0, unroll=2)


def third_kernel(s_ref, zlo_ref, zhi_ref, out_ref):
    planes, height, length = s_ref.shape

    def one(i, carry):
        gap = jnp.zeros((LANES - 4, height), F32)
        side = jnp.concatenate([zhi_ref[i], gap, zlo_ref[i]], axis=0).T
        t = jnp.concatenate([s_ref[i], side], axis=1)
        out_ref[i] = box(box(t, 1), 1)[:, 0:length]
        return carry

    lax.fori_loop(0, planes, one, 0, unroll=2)


VMEM = pl.BlockSpec(memory_space=pltpu.VMEM)
SMEM = pl.BlockSpec(memory_space=pltpu.SMEM)


def on_device(displacement, density, stiffness):
    planes, height, length = density.shape
    sizes = tuple(lax.axis_size(a) for a in AXES)
    devices = sizes[0] * sizes[1] * sizes[2]
    extents = tuple(n * s for n, s in zip(density.shape, sizes))
    where = jnp.stack([lax.axis_index(a) for a in AXES]).astype(jnp.int32)

    def shape(*dims):
        return jax.ShapeDtypeStruct(dims, F32)

    zcol = jnp.pad(displacement[..., 0].transpose(1, 0, 2), ((0, 0), (0, 0), (0, LANES - height)))
    zh = shift_from(zcol, "gz", 1)
    xh = shift_from(displacement[:, :1], "gx", 1)
    yrow = jnp.concatenate([displacement[:, :, 0], zh[:, :, :1].transpose(1, 0, 2)], axis=2)
    yh = shift_from(yrow, "gy", 1)
    edge = jnp.concatenate(
        [yh[:, 0], jnp.zeros((3, LANES - 1), F32), zh[0]], axis=1
    )
    edge = shift_from(edge, "gx", 1)

    side = 24 * ROWS
    gains, inverse = pl.pallas_call(
        functools.partial(setup_kernel, extents=extents),
        in_specs=[SMEM, VMEM],
        out_specs=[VMEM, VMEM],
        out_shape=[jax.ShapeDtypeStruct((2 * side, side), BF16), shape(height, length)],
        name="setup",
    )(where, stiffness)
    corner_space = pltpu.VMEM((2, 12, height, length), F32)
    weighted, low, part = pl.pallas_call(
        functools.partial(main_kernel, extent=extents[0]),
        in_specs=[SMEM] + [VMEM] * 6,
        out_specs=[VMEM] * 3,
        out_shape=[shape(planes, height, length), shape(2, height, length), shape(2, ROWS, length)],
        scratch_shapes=[corner_space],
        name="energy",
    )(where, displacement, yh, zh, density, gains, inverse)
    xhi = shift_from(low, "gx", 1)

    def whole(array):
        return pl.BlockSpec(array.shape, lambda i: (0,) * array.ndim)

    def plane_of(at):
        return pl.BlockSpec((1, height, length), lambda i: (at, 0, 0))

    high, sums = pl.pallas_call(
        functools.partial(last_kernel, extent=extents[0], planes=planes),
        grid=(1,),
        in_specs=[
            SMEM,
            pl.BlockSpec((3, 1, height, length), lambda i: (0, planes - 1, 0, 0)),
            whole(xh),
            whole(edge),
            whole(yh),
            whole(zh),
            plane_of(planes - 1),
            whole(gains),
            whole(inverse),
            plane_of(planes - 2),
            whole(part),
        ],
        out_specs=[
            pl.BlockSpec((2, height, length), lambda i: (0, 0, 0)),
            pl.BlockSpec((devices, 1, LANES), lambda i: (0, 0, 0)),
        ],
        out_shape=[shape(2, height, length), shape(devices, 1, LANES)],
        scratch_shapes=[corner_space],
        name="energy_last",
    )(where, displacement, xh, edge, yh, zh, density, gains, inverse, weighted, part)

    xlo = shift_from(high, "gx", -1)
    gathered = lax.all_to_all(sums, AXES, 0, 0, tiled=True)
    totals = jnp.sum(gathered, axis=(0, 1))

    rows = 1 if sizes[1] == 2 else 2
    smooth_x = pl.pallas_call(
        first_kernel,
        in_specs=[SMEM] + [VMEM] * 4,
        out_specs=[VMEM] * (1 + rows),
        out_shape=[shape(planes, height, length)] + [shape(planes, 2, length)] * rows,
        name="along_x",
    )
    smooth, *parts = smooth_x(where, weighted, high, xlo, xhi)
    if rows == 1:
        parts = [lax.ppermute(parts[0], "gy", [(0, 1), (1, 0)])]
    else:
        parts = [shift_from(parts[1], "gy", -1), shift_from(parts[0], "gy", 1)]
    smooth, low, high = pl.pallas_call(
        second_kernel,
        in_specs=[SMEM] + [VMEM] * (1 + rows),
        out_specs=[VMEM] * 3,
        out_shape=[shape(planes, height, length)] + [shape(planes, 2, height)] * 2,
        name="along_y",
    )(where, smooth, *parts)
    zlo = shift_from(high, "gz", -1)
    zhi = shift_from(low, "gz", 1)
    filtered = pl.pallas_call(
        third_kernel,
        in_specs=[VMEM] * 3,
        out_specs=VMEM,
        out_shape=shape(planes, height, length),
        name="along_z",
    )(smooth, zlo, zhi)

    cells = float(extents[0] * extents[1] * extents[2])
    return filtered, totals[0] / cells, totals[1] / cells


def solution(mesh):
    return jax.shard_map(
        on_device,
        mesh=mesh,
        in_specs=(P(None, *AXES), P(*AXES), P()),
        out_specs=(P(*AXES), P(), P()),
        check_vma=False,
    )
```

time: 76.3 us -> 77.9 us (1.021)
  waiting for transfers between devices: 14.4 us -> 9.79 us
  blocking collectives: 11.5 us -> 15.9 us
  Pallas kernels: 21.8 us -> 25.4 us
  local copies, waits for them, and re-layouts: 6.48 us -> 4.79 us
    ppermute x7 -> x8, waiting for transfers between devices: 14.4 us -> 9.79 us  [shift_from(): return lax.ppermute(block, axis, route)]
    all_to_all x1, blocking collectives: 11.5 us -> 15.9 us  [on_device(): gathered = lax.all_to_all(sums, AXES, 0, 0, tiled=True)]
    pallas_call x2 -> x4, Pallas kernels: 14.5 us -> 18.1 us  [the longest x1 11.7 us: on_device(): pl.pallas_call(functools.partial(main_kernel, extent=extents[0]), in_spec...]
    ppermute x2 -> x0, local copies, waits for them, and re-layouts: 1.31 us -> none  [shift_from(): return lax.ppermute(block, axis, route)]
    slice x1, local copies, waits for them, and re-layouts: 0.98 us -> 0.01 us  [on_device(): xh = shift_from(displacement[:, :1], 'gx', 1)]
    unnamed x13 -> x23, local copies, waits for them, and re-layouts: 2.38 us -> 2.94 us
    ppermute x7 -> x8, starting transfers between devices: 16 us -> 16.3 us  [shift_from(): return lax.ppermute(block, axis, route)]
  transfers between devices with their start and end apart: 8 -> 9, of which waited for: 6 -> 4; matrix products, arithmetic and copies ran while one was open for 6% -> 2% of each run, Pallas kernels for 0% -> 21%
where the time goes in v3:
time: 77.9 us; the launch traced here: 77.4 us
  Pallas kernels  25.4 us (33%)
  starting transfers between devices  16.3 us (21%)
  blocking collectives  15.9 us (20%)
  waiting for transfers between devices  9.79 us (13%)
  local copies, waits for them, and re-layouts  4.79 us (6%)
  between operations  4.45 us (6%)
    ppermute x8, starting transfers between devices, shift_from(): return lax.ppermute(block, axis, route)  16.3 us
    all_to_all x1, blocking collectives, on_device(): gathered = lax.all_to_all(sums, AXES, 0, 0, tiled=True)  15.9 us
    pallas_call x1, Pallas kernels, on_device(): pl.pallas_call(functools.partial(main_kernel, extent=extents[0]), in_spec...  11.7 us
    ppermute x8, waiting for transfers between devices, shift_from(): return lax.ppermute(block, axis, route)  9.79 us
    pallas_call x1, Pallas kernels, on_device(): pl.pallas_call(third_kernel, in_specs=[VMEM] * 3, out_specs=VMEM, out_sha...  4.55 us
    unnamed x23, local copies, waits for them, and re-layouts  2.94 us
    pallas_call x1, Pallas kernels, on_device(): pl.pallas_call(second_kernel, in_specs=[SMEM] + [VMEM] * (1 + rows), out_...  2.75 us
    pallas_call x1, Pallas kernels, on_device(): pl.pallas_call(functools.partial(last_kernel, extent=extents[0], planes=p...  2.65 us
  transfers between devices with their start and end apart: 9, of which 4 were waited for; matrix products, arithmetic and copies ran while one was open for 2% of the time, Pallas kernels for 21%

profile of v3, /device:TPU:1, one launch (start us, length us, event | category | flops | bytes accessed | tf_op | source)
XLA Modules:
  0.0 77.4 jit_solution(13400990160088939093)
XLA Ops:
  0.7 1.1 %slice-done = f32[3,16,32,1]{3,2,1,0:T(8,128)S(1)} async-done(((f32[3,16,32,256]{3,2,1,0:T(8,128)}), f32[3,16,32,1]{3,2,1,0:T(8,128)S(1)}, s32[]{:S(2)}) %slice-start) | async-done | bytes 6168 | tf_op jit(solution)/shard_map/slice | solution.py:253
  2.2 1.9 %collective-permute-start = (f32[16,3,128]{2,1,0:T(4,128)S(1)}, f32[16,3,128]{2,1,0:T(4,128)S(1)}, u32[]{:S(2)}, u32[]{:S(2)}) collective-permute-start(f32[16,3,128]{2,1,0:T(4,128)S(1)} %pad.4), channel_id=1, source_target_pairs={{1,0},{2,1},{3,2},{5,4},{6,5},{7,6},{9,8},{10,9},{11,10},{13,12},{... | collective-permute-start | bytes 73736 | tf_op jit(solution)/shard_map/ppermute | solution.py:22
  4.2 1.3 %collective-permute-start.2 = (f32[3,1,32,256]{3,2,1,0:T(8,128)S(1)}, f32[3,1,32,256]{3,2,1,0:T(8,128)S(1)}, u32[]{:S(2)}, u32[]{:S(2)}) collective-permute-start(f32[3,1,32,256]{3,2,1,0:T(8,128)S(1)} %slice.27), channel_id=1, source_target_pairs={{8,0},{16,8},{24,16},{9,1},{17,9},{25,17},{10,2},{18,10},{26,18},{... | collective-permute-start | bytes 294920 | tf_op jit(solution)/shard_map/ppermute | solution.py:22
  5.6 2.7 %collective-permute-done.zh_ref = f32[16,3,128]{2,1,0:T(4,128)S(1)} collective-permute-done((f32[16,3,128]{2,1,0:T(4,128)S(1)}, f32[16,3,128]{2,1,0:T(4,128)S(1)}, u32[]{:S(2)}, u32[]{:S(2)}) %collective-permute-start) | collective-permute-done | bytes 24608 | tf_op jit(solution)/shard_map/ppermute | solution.py:22
  8.4 1.3 %collective-permute-start.1 = (f32[3,16,257]{2,1,0:T(8,128)S(1)}, f32[3,16,257]{2,1,0:T(8,128)S(1)}, u32[]{:S(2)}, u32[]{:S(2)}) collective-permute-start(f32[3,16,257]{2,1,0:T(8,128)S(1)} %pad_maximum_fusion), channel_id=1, source_target_pairs={{4,0},{5,1},{6,2},{7,3},{12,8},{13,9},{14,10},{15,11},{20,16},{21,... | collective-permute-start | bytes 148040 | tf_op jit(solution)/shard_map/ppermute | solution.py:22
  9.7 3.8 %collective-permute-done.1.yh_ref = f32[3,16,257]{2,1,0:T(8,128)S(1)} collective-permute-done((f32[3,16,257]{2,1,0:T(8,128)S(1)}, f32[3,16,257]{2,1,0:T(8,128)S(1)}, u32[]{:S(2)}, u32[]{:S(2)}) %collective-permute-start.1) | collective-permute-done | bytes 49376 | tf_op jit(solution)/shard_map/ppermute | solution.py:22
  13.5 1.3 %collective-permute-start.3 = (f32[3,512]{1,0:T(4,128)S(1)}, f32[3,512]{1,0:T(4,128)S(1)}, u32[]{:S(2)}, u32[]{:S(2)}) collective-permute-start(f32[3,512]{1,0:T(4,128)S(1)} %pad_maximum_fusion.1), channel_id=1, source_target_pairs={{8,0},{16,8},{24,16},{9,1},{17,9},{25,17},{10,2},{18,10},{26,18},{... | collective-permute-start | bytes 18440 | tf_op jit(solution)/shard_map/ppermute | solution.py:22
  14.8 0.7 pad_add_fusion.where_ref
  15.4 1.7 %setup.1 = (bf16[384,192]{1,0:T(8,128)(2,1)}, f32[32,256]{1,0:T(8,128)}) custom-call(s32[3]{0:T(128)} %pad_add_fusion.where_ref, f32[24,24]{1,0:T(8,128)} %k_ref.1), custom_call_target="tpu_custom_call" | custom-call | tf_op jit(solution)/shard_map/setup/pallas_call | solution.py:264
  17.2 11.7 %energy.1 = (f32[16,32,256]{2,1,0:T(8,128)}, f32[2,32,256]{2,1,0:T(8,128)}, f32[2,8,256]{2,1,0:T(8,128)}) custom-call(s32[3]{0:T(128)} %pad_add_fusion.where_ref, f32[3,16,32,256]{3,2,1,0:T(8,128)} %u_ref.3, f32[3,16,257]{2,1,0:T(8,128)} %copy-done.1, f32[16,3,128]{2,1,0:T(4,128)} %copy-done.2, f32[16,32,256]{2,1,0:T(8,128)} %rho_ref.3, ...), custom_call_target="tpu_custom_call" | custom-call | tf_op jit(solution)/shard_map/energy/pallas_call | solution.py:272
  28.9 1.3 %collective-permute-start.5 = (f32[2,32,256]{2,1,0:T(8,128)}, f32[2,32,256]{2,1,0:T(8,128)S(1)}, u32[]{:S(2)}, u32[]{:S(2)}) collective-permute-start(f32[2,32,256]{2,1,0:T(8,128)} %get-tuple-element.20), channel_id=1, source_target_pairs={{8,0},{16,8},{24,16},{9,1},{17,9},{25,17},{10,2},{18,10},{26,18},{... | collective-permute-start | bytes 196616 | tf_op jit(solution)/shard_map/ppermute | solution.py:22
  30.8 2.7 %energy_last.1 = (f32[2,32,256]{2,1,0:T(8,128)}, f32[32,1,128]{2,1,0:T(1,128)}) custom-call(s32[3]{0:T(128)} %pad_add_fusion.where_ref, f32[3,16,32,256]{3,2,1,0:T(8,128)} %u_ref.3, f32[3,1,32,256]{3,2,1,0:T(8,128)} %copy-done.3, f32[3,512]{1,0:T(4,128)} %copy-done.9, f32[3,16,257]{2,1,0:T(8,128)} %copy-done.1, f32[16,3,128]{2,1,0:T(4,128)} %copy-done.2, ...), custom_call_target="tpu_custom_call" | custom-call | tf_op jit(solution)/shard_map/energy_last/pallas_call | solution.py:288
  33.5 4.6 %collective-permute-start.4 = (f32[2,32,256]{2,1,0:T(8,128)}, f32[2,32,256]{2,1,0:T(8,128)S(1)}, u32[]{:S(2)}, u32[]{:S(2)}) collective-permute-start(f32[2,32,256]{2,1,0:T(8,128)} %get-tuple-element.19.own_ref), channel_id=1, source_target_pairs={{0,8},{8,16},{16,24},{1,9},{9,17},{17,25},{2,10},{10,18},{18,26},{... | collective-permute-start | bytes 196616 | tf_op jit(solution)/shard_map/ppermute | solution.py:22
  38.1 1.9 %collective-permute-done.4.xlo_ref = f32[2,32,256]{2,1,0:T(8,128)S(1)} collective-permute-done((f32[2,32,256]{2,1,0:T(8,128)}, f32[2,32,256]{2,1,0:T(8,128)S(1)}, u32[]{:S(2)}, u32[]{:S(2)}) %collective-permute-start.4) | collective-permute-done | bytes 65568 | tf_op jit(solution)/shard_map/ppermute | solution.py:22
  40.0 0.6 copy-done.5
  40.6 2.0 %along_x.1 = (f32[16,32,256]{2,1,0:T(8,128)}, f32[16,2,256]{2,1,0:T(2,128)}) custom-call(s32[3]{0:T(128)} %pad_add_fusion.where_ref, f32[16,32,256]{2,1,0:T(8,128)} %get-tuple-element.17.w_ref, f32[2,32,256]{2,1,0:T(8,128)} %get-tuple-element.19.own_ref, f32[2,32,256]{2,1,0:T(8,128)} %copy-done.5, f32[2,32,256]{2,1,0:T(8,128)} %copy-done.4), custom_call_target="tpu_custom_call" | custom-call | tf_op jit(solution)/shard_map/along_x/pallas_call | solution.py:325
  42.7 15.9 %all_to_all.5 = f32[32,1,128]{2,1,0:T(1,128)S(1)} all-to-all(f32[32,1,128]{2,1,0:T(1,128)} %get-tuple-element.26), channel_id=1, replica_groups=mesh['gx'=4,'gy'=2,'gz'=4] {'gx','gy','gz'}, dimensions={0} | all-to-all | bytes 32768 | tf_op jit(solution)/shard_map/all_to_all | solution.py:314
  58.7 0.6 copy-done.6
  59.3 2.7 %along_y.1 = (f32[16,32,256]{2,1,0:T(8,128)}, f32[16,2,32]{2,1,0:T(2,128)}, f32[16,2,32]{2,1,0:T(2,128)}) custom-call(s32[3]{0:T(128)} %pad_add_fusion.where_ref, f32[16,32,256]{2,1,0:T(8,128)} %get-tuple-element.21.s_ref, f32[16,2,256]{2,1,0:T(2,128)} %copy-done.6), custom_call_target="tpu_custom_call" | custom-call | tf_op jit(solution)/shard_map/along_y/pallas_call | solution.py:330
  62.0 2.7 %collective-permute-start.7 = (f32[16,2,32]{2,1,0:T(2,128)}, f32[16,2,32]{2,1,0:T(2,128)S(1)}, u32[]{:S(2)}, u32[]{:S(2)}) collective-permute-start(f32[16,2,32]{2,1,0:T(2,128)} %get-tuple-element.24), channel_id=1, source_target_pairs={{0,1},{1,2},{2,3},{4,5},{5,6},{6,7},{8,9},{9,10},{10,11},{12,13},{... | collective-permute-start | bytes 12296 | tf_op jit(solution)/shard_map/ppermute | solution.py:22
  64.7 1.9 %collective-permute-start.8 = (f32[16,2,32]{2,1,0:T(2,128)}, f32[16,2,32]{2,1,0:T(2,128)S(1)}, u32[]{:S(2)}, u32[]{:S(2)}) collective-permute-start(f32[16,2,32]{2,1,0:T(2,128)} %get-tuple-element.25), channel_id=1, source_target_pairs={{1,0},{2,1},{3,2},{5,4},{6,5},{7,6},{9,8},{10,9},{11,10},{13,12},{... | collective-permute-start | bytes 12296 | tf_op jit(solution)/shard_map/ppermute | solution.py:22
  68.5 1.4 %collective-permute-done.8.zhi_ref = f32[16,2,32]{2,1,0:T(2,128)S(1)} collective-permute-done((f32[16,2,32]{2,1,0:T(2,128)}, f32[16,2,32]{2,1,0:T(2,128)S(1)}, u32[]{:S(2)}, u32[]{:S(2)}) %collective-permute-start.8) | collective-permute-done | bytes 4128 | tf_op jit(solution)/shard_map/ppermute | solution.py:22
  70.0 0.6 copy-done.8
  70.6 4.5 %along_z.1 = f32[16,32,256]{2,1,0:T(8,128)} custom-call(f32[16,32,256]{2,1,0:T(8,128)} %get-tuple-element.23.s_ref, f32[16,2,32]{2,1,0:T(2,128)} %copy-done.7, f32[16,2,32]{2,1,0:T(2,128)} %copy-done.8), custom_call_target="tpu_custom_call" | custom-call | tf_op jit(solution)/shard_map/along_z/pallas_call | solution.py:339
  (40 shorter events, 1.9 us)
Async XLA Ops:
  0.6 1.1 %slice-start = ((f32[3,16,32,256]{3,2,1,0:T(8,128)}), f32[3,16,32,1]{3,2,1,0:T(8,128)S(1)}, s32[]{:S(2)}) async-start(f32[3,16,32,256]{3,2,1,0:T(8,128)} %u_ref.3), calls=%async_computation.1 | async-start | bytes 1572864 | tf_op jit(solution)/shard_map/slice | solution.py:253
  0.6 3.5 %copy-start = (f32[3,16,32,256]{3,2,1,0:T(8,128)S(1)}, f32[3,16,32,256]{3,2,1,0:T(8,128)}, u32[]{:S(2)}) copy-start(f32[3,16,32,256]{3,2,1,0:T(8,128)} %u_ref.3) | copy-start | bytes 4718596
  2.2 6.1 %collective-permute-start = (f32[16,3,128]{2,1,0:T(4,128)S(1)}, f32[16,3,128]{2,1,0:T(4,128)S(1)}, u32[]{:S(2)}, u32[]{:S(2)}) collective-permute-start(f32[16,3,128]{2,1,0:T(4,128)S(1)} %pad.4), channel_id=1, source_target_pairs={{1,0},{2,1},{3,2},{5,4},{6,5},{7,6},{9,8},{10,9},{11,10},{13,12},{... | collective-permute-start | bytes 73736 | tf_op jit(solution)/shard_map/ppermute | solution.py:22
  4.2 26.0 %collective-permute-start.2 = (f32[3,1,32,256]{3,2,1,0:T(8,128)S(1)}, f32[3,1,32,256]{3,2,1,0:T(8,128)S(1)}, u32[]{:S(2)}, u32[]{:S(2)}) collective-permute-start(f32[3,1,32,256]{3,2,1,0:T(8,128)S(1)} %slice.27), channel_id=1, source_target_pairs={{8,0},{16,8},{24,16},{9,1},{17,9},{25,17},{10,2},{18,10},{26,18},{... | collective-permute-start | bytes 294920 | tf_op jit(solution)/shard_map/ppermute | solution.py:22
  8.3 8.8 %copy-start.2 = (f32[16,3,128]{2,1,0:T(4,128)}, f32[16,3,128]{2,1,0:T(4,128)S(1)}, u32[]{:S(2)}) copy-start(f32[16,3,128]{2,1,0:T(4,128)S(1)} %collective-permute-done.zh_ref) | copy-start | bytes 73732
  8.4 5.1 %collective-permute-start.1 = (f32[3,16,257]{2,1,0:T(8,128)S(1)}, f32[3,16,257]{2,1,0:T(8,128)S(1)}, u32[]{:S(2)}, u32[]{:S(2)}) collective-permute-start(f32[3,16,257]{2,1,0:T(8,128)S(1)} %pad_maximum_fusion), channel_id=1, source_target_pairs={{4,0},{5,1},{6,2},{7,3},{12,8},{13,9},{14,10},{15,11},{20,16},{21,... | collective-permute-start | bytes 148040 | tf_op jit(solution)/shard_map/ppermute | solution.py:22
  13.5 3.7 %copy-start.1 = (f32[3,16,257]{2,1,0:T(8,128)}, f32[3,16,257]{2,1,0:T(8,128)S(1)}, u32[]{:S(2)}) copy-start(f32[3,16,257]{2,1,0:T(8,128)S(1)} %collective-permute-done.1.yh_ref) | copy-start | bytes 148036
  13.5 16.7 %collective-permute-start.3 = (f32[3,512]{1,0:T(4,128)S(1)}, f32[3,512]{1,0:T(4,128)S(1)}, u32[]{:S(2)}, u32[]{:S(2)}) collective-permute-start(f32[3,512]{1,0:T(4,128)S(1)} %pad_maximum_fusion.1), channel_id=1, source_target_pairs={{8,0},{16,8},{24,16},{9,1},{17,9},{25,17},{10,2},{18,10},{26,18},{... | collective-permute-start | bytes 18440 | tf_op jit(solution)/shard_map/ppermute | solution.py:22
  28.9 9.2 %collective-permute-start.5 = (f32[2,32,256]{2,1,0:T(8,128)}, f32[2,32,256]{2,1,0:T(8,128)S(1)}, u32[]{:S(2)}, u32[]{:S(2)}) collective-permute-start(f32[2,32,256]{2,1,0:T(8,128)} %get-tuple-element.20), channel_id=1, source_target_pairs={{8,0},{16,8},{24,16},{9,1},{17,9},{25,17},{10,2},{18,10},{26,18},{... | collective-permute-start | bytes 196616 | tf_op jit(solution)/shard_map/ppermute | solution.py:22
  30.2 0.6 copy-start.9
  30.2 0.6 copy-start.3
  33.5 6.5 %collective-permute-start.4 = (f32[2,32,256]{2,1,0:T(8,128)}, f32[2,32,256]{2,1,0:T(8,128)S(1)}, u32[]{:S(2)}, u32[]{:S(2)}) collective-permute-start(f32[2,32,256]{2,1,0:T(8,128)} %get-tuple-element.19.own_ref), channel_id=1, source_target_pairs={{0,8},{8,16},{16,24},{1,9},{9,17},{17,25},{2,10},{10,18},{18,26},{... | collective-permute-start | bytes 196616 | tf_op jit(solution)/shard_map/ppermute | solution.py:22
  38.1 1.9 %copy-start.4 = (f32[2,32,256]{2,1,0:T(8,128)}, f32[2,32,256]{2,1,0:T(8,128)S(1)}, u32[]{:S(2)}) copy-start(f32[2,32,256]{2,1,0:T(8,128)S(1)} %collective-permute-done.5.xhi_ref) | copy-start | bytes 196612
  40.0 0.6 copy-start.5
  42.7 16.0 %collective-permute-start.6 = (f32[16,2,256]{2,1,0:T(2,128)}, f32[16,2,256]{2,1,0:T(2,128)S(1)}, u32[]{:S(2)}, u32[]{:S(2)}) collective-permute-start(f32[16,2,256]{2,1,0:T(2,128)} %get-tuple-element.22), channel_id=1, source_target_pairs={{0,4},{4,0},{1,5},{5,1},{2,6},{6,2},{3,7},{7,3},{8,12},{12,8},{9,1... | collective-permute-start | bytes 98312 | tf_op jit(solution)/shard_map/ppermute | solution.py:327
  58.7 0.6 copy-start.6
  62.0 6.5 %collective-permute-start.7 = (f32[16,2,32]{2,1,0:T(2,128)}, f32[16,2,32]{2,1,0:T(2,128)S(1)}, u32[]{:S(2)}, u32[]{:S(2)}) collective-permute-start(f32[16,2,32]{2,1,0:T(2,128)} %get-tuple-element.24), channel_id=1, source_target_pairs={{0,1},{1,2},{2,3},{4,5},{5,6},{6,7},{8,9},{9,10},{10,11},{12,13},{... | collective-permute-start | bytes 12296 | tf_op jit(solution)/shard_map/ppermute | solution.py:22
  64.7 5.3 %collective-permute-start.8 = (f32[16,2,32]{2,1,0:T(2,128)}, f32[16,2,32]{2,1,0:T(2,128)S(1)}, u32[]{:S(2)}, u32[]{:S(2)}) collective-permute-start(f32[16,2,32]{2,1,0:T(2,128)} %get-tuple-element.25), channel_id=1, source_target_pairs={{1,0},{2,1},{3,2},{5,4},{6,5},{7,6},{9,8},{10,9},{11,10},{13,12},{... | collective-permute-start | bytes 12296 | tf_op jit(solution)/shard_map/ppermute | solution.py:22
  68.5 1.4 %copy-start.7 = (f32[16,2,32]{2,1,0:T(2,128)}, f32[16,2,32]{2,1,0:T(2,128)S(1)}, u32[]{:S(2)}) copy-start(f32[16,2,32]{2,1,0:T(2,128)S(1)} %collective-permute-done.7.zlo_ref) | copy-start | bytes 12292
  70.0 0.6 copy-start.8

commit v4 on v3

--- a/solution.py
+++ b/solution.py
@@ -204,36 +204,37 @@
 def second_kernel(where_ref, s_ref, *refs):
     planes, height, length = s_ref.shape
     messages, (out_ref, low_ref, high_ref) = refs[:-3], refs[-3:]
-
-    def one(i, carry):
-        if len(messages) == 1:
-            got = messages[0][i]
-            before = jnp.where(where_ref[1] == 1, got, 0.0)
-            after = jnp.where(where_ref[1] == 0, got, 0.0)
-        else:
-            before, after = messages[0][i], messages[1][i]
-        gap = jnp.zeros((ROWS - 4, length), F32)
-        t = jnp.concatenate([s_ref[i], after, gap, before], axis=0)
-        t = box(box(t, 0), 0)[0:height]
-        out_ref[i] = t
-        low_ref[i] = t[:, 0:LANES].T[0:2]
-        high_ref[i] = t[:, length - LANES : length].T[LANES - 2 : LANES]
-        return carry
-
-    lax.fori_loop(0, planes, one, 0, unroll=2)
+    group = LANES // height
+    gap = jnp.zeros((ROWS - 4, length), F32)
+    for g in range(planes // group):
+        done = []
+        for i in range(g * group, (g + 1) * group):
+            if len(messages) == 1:
+                got = messages[0][i]
+                before = jnp.where(where_ref[1] == 1, got, 0.0)
+                after = jnp.where(where_ref[1] == 0, got, 0.0)
+            else:
+                before, after = messages[0][i], messages[1][i]
+            t = jnp.concatenate([s_ref[i], after, gap, before], axis=0)
+            t = box(box(t, 0), 0)[0:height]
+            out_ref[i] = t
+            done.append(t)
+        at = slice(g * LANES, (g + 1) * LANES)
+        low_ref[:, at] = jnp.concatenate([t[:, 0:LANES] for t in done], axis=0).T[0:2]
+        high_ref[:, at] = jnp.concatenate([t[:, length - LANES :] for t in done], axis=0).T[LANES - 2 :]
 
 
 def third_kernel(s_ref, zlo_ref, zhi_ref, out_ref):
     planes, height, length = s_ref.shape
-
-    def one(i, carry):
-        gap = jnp.zeros((LANES - 4, height), F32)
-        side = jnp.concatenate([zhi_ref[i], gap, zlo_ref[i]], axis=0).T
-        t = jnp.concatenate([s_ref[i], side], axis=1)
-        out_ref[i] = box(box(t, 1), 1)[:, 0:length]
-        return carry
-
-    lax.fori_loop(0, planes, one, 0, unroll=2)
+    group = LANES // height
+    gap = jnp.zeros((LANES - 4, LANES), F32)
+    for g in range(planes // group):
+        at = slice(g * LANES, (g + 1) * LANES)
+        side = jnp.concatenate([zhi_ref[:, at], gap, zlo_ref[:, at]], axis=0).T
+        for k in range(group):
+            i = g * group + k
+            t = jnp.concatenate([s_ref[i], side[k * height : (k + 1) * height]], axis=1)
+            out_ref[i] = box(box(t, 1), 1)[:, 0:length]
 
 
 VMEM = pl.BlockSpec(memory_space=pltpu.VMEM)
@@ -261,13 +262,14 @@
     edge = shift_from(edge, "gx", 1)
 
     side = 24 * ROWS
-    gains, inverse = pl.pallas_call(
+    setup = pl.pallas_call(
         functools.partial(setup_kernel, extents=extents),
         in_specs=[SMEM, VMEM],
         out_specs=[VMEM, VMEM],
         out_shape=[jax.ShapeDtypeStruct((2 * side, side), BF16), shape(height, length)],
         name="setup",
-    )(where, stiffness)
+    )
+    gains, inverse = setup(where, stiffness)
     corner_space = pltpu.VMEM((2, 12, height, length), F32)
     weighted, low, part = pl.pallas_call(
         functools.partial(main_kernel, extent=extents[0]),
@@ -331,7 +333,7 @@
         second_kernel,
         in_specs=[SMEM] + [VMEM] * (1 + rows),
         out_specs=[VMEM] * 3,
-        out_shape=[shape(planes, height, length)] + [shape(planes, 2, height)] * 2,
+        out_shape=[shape(planes, height, length)] + [shape(2, planes * height)] * 2,
         name="along_y",
     )(where, smooth, *parts)
     zlo = shift_from(high, "gz", -1)

time: 77.9 us -> 76.3 us (0.979)
  Pallas kernels: 25.4 us -> 24 us
    pallas_call x1, Pallas kernels: 4.55 us -> 3.7 us  [on_device(): pl.pallas_call(third_kernel, in_specs=[VMEM] * 3, out_specs=VMEM, out_sha...]
where the time goes in v4:
time: 76.3 us; the launch traced here: 75.8 us
  Pallas kernels  24 us (31%)
  starting transfers between devices  16.3 us (21%)
  blocking collectives  15.9 us (21%)
  waiting for transfers between devices  9.66 us (13%)
  local copies, waits for them, and re-layouts  4.78 us (6%)
  between operations  4.45 us (6%)
    ppermute x8, starting transfers between devices, shift_from(): return lax.ppermute(block, axis, route)  16.3 us
    all_to_all x1, blocking collectives, on_device(): gathered = lax.all_to_all(sums, AXES, 0, 0, tiled=True)  15.9 us
    pallas_call x1, Pallas kernels, on_device(): pl.pallas_call(functools.partial(main_kernel, extent=extents[0]), in_spec...  11.7 us
    ppermute x8, waiting for transfers between devices, shift_from(): return lax.ppermute(block, axis, route)  9.65 us
    pallas_call x1, Pallas kernels, on_device(): pl.pallas_call(third_kernel, in_specs=[VMEM] * 3, out_specs=VMEM, out_sha...  3.7 us
    unnamed x23, local copies, waits for them, and re-layouts  2.93 us
    pallas_call x1, Pallas kernels, on_device(): pl.pallas_call(functools.partial(last_kernel, extent=extents[0], planes=p...  2.65 us
    pallas_call x1, Pallas kernels, on_device(): pl.pallas_call(second_kernel, in_specs=[SMEM] + [VMEM] * (1 + rows), out_...  2.13 us
  transfers between devices with their start and end apart: 9, of which 4 were waited for; matrix products, arithmetic and copies ran while one was open for 2% of the time, Pallas kernels for 21%

profile of v4, /device:TPU:1, one launch (start us, length us, event | category | flops | bytes accessed | tf_op | source)
XLA Modules:
  0.0 75.8 jit_solution(168657731779414212)
XLA Ops:
  0.7 1.1 %slice-done = f32[3,16,32,1]{3,2,1,0:T(8,128)S(1)} async-done(((f32[3,16,32,256]{3,2,1,0:T(8,128)}), f32[3,16,32,1]{3,2,1,0:T(8,128)S(1)}, s32[]{:S(2)}) %slice-start) | async-done | bytes 6168 | tf_op jit(solution)/shard_map/slice | solution.py:254
  2.2 1.9 %collective-permute-start = (f32[16,3,128]{2,1,0:T(4,128)S(1)}, f32[16,3,128]{2,1,0:T(4,128)S(1)}, u32[]{:S(2)}, u32[]{:S(2)}) collective-permute-start(f32[16,3,128]{2,1,0:T(4,128)S(1)} %pad.4), channel_id=1, source_target_pairs={{1,0},{2,1},{3,2},{5,4},{6,5},{7,6},{9,8},{10,9},{11,10},{13,12},{... | collective-permute-start | bytes 73736 | tf_op jit(solution)/shard_map/ppermute | solution.py:22
  4.2 1.3 %collective-permute-start.2 = (f32[3,1,32,256]{3,2,1,0:T(8,128)S(1)}, f32[3,1,32,256]{3,2,1,0:T(8,128)S(1)}, u32[]{:S(2)}, u32[]{:S(2)}) collective-permute-start(f32[3,1,32,256]{3,2,1,0:T(8,128)S(1)} %slice.27), channel_id=1, source_target_pairs={{8,0},{16,8},{24,16},{9,1},{17,9},{25,17},{10,2},{18,10},{26,18},{... | collective-permute-start | bytes 294920 | tf_op jit(solution)/shard_map/ppermute | solution.py:22
  5.6 2.7 %collective-permute-done.zh_ref = f32[16,3,128]{2,1,0:T(4,128)S(1)} collective-permute-done((f32[16,3,128]{2,1,0:T(4,128)S(1)}, f32[16,3,128]{2,1,0:T(4,128)S(1)}, u32[]{:S(2)}, u32[]{:S(2)}) %collective-permute-start) | collective-permute-done | bytes 24608 | tf_op jit(solution)/shard_map/ppermute | solution.py:22
  8.4 1.3 %collective-permute-start.1 = (f32[3,16,257]{2,1,0:T(8,128)S(1)}, f32[3,16,257]{2,1,0:T(8,128)S(1)}, u32[]{:S(2)}, u32[]{:S(2)}) collective-permute-start(f32[3,16,257]{2,1,0:T(8,128)S(1)} %pad_maximum_fusion), channel_id=1, source_target_pairs={{4,0},{5,1},{6,2},{7,3},{12,8},{13,9},{14,10},{15,11},{20,16},{21,... | collective-permute-start | bytes 148040 | tf_op jit(solution)/shard_map/ppermute | solution.py:22
  9.7 3.8 %collective-permute-done.1.yh_ref = f32[3,16,257]{2,1,0:T(8,128)S(1)} collective-permute-done((f32[3,16,257]{2,1,0:T(8,128)S(1)}, f32[3,16,257]{2,1,0:T(8,128)S(1)}, u32[]{:S(2)}, u32[]{:S(2)}) %collective-permute-start.1) | collective-permute-done | bytes 49376 | tf_op jit(solution)/shard_map/ppermute | solution.py:22
  13.5 1.3 %collective-permute-start.3 = (f32[3,512]{1,0:T(4,128)S(1)}, f32[3,512]{1,0:T(4,128)S(1)}, u32[]{:S(2)}, u32[]{:S(2)}) collective-permute-start(f32[3,512]{1,0:T(4,128)S(1)} %pad_maximum_fusion.1), channel_id=1, source_target_pairs={{8,0},{16,8},{24,16},{9,1},{17,9},{25,17},{10,2},{18,10},{26,18},{... | collective-permute-start | bytes 18440 | tf_op jit(solution)/shard_map/ppermute | solution.py:22
  14.8 0.7 pad_add_fusion.where_ref
  15.4 1.7 %setup.1 = (bf16[384,192]{1,0:T(8,128)(2,1)}, f32[32,256]{1,0:T(8,128)}) custom-call(s32[3]{0:T(128)} %pad_add_fusion.where_ref, f32[24,24]{1,0:T(8,128)} %k_ref.1), custom_call_target="tpu_custom_call" | custom-call | tf_op jit(solution)/shard_map/setup/pallas_call | solution.py:272
  17.2 11.7 %energy.1 = (f32[16,32,256]{2,1,0:T(8,128)}, f32[2,32,256]{2,1,0:T(8,128)}, f32[2,8,256]{2,1,0:T(8,128)}) custom-call(s32[3]{0:T(128)} %pad_add_fusion.where_ref, f32[3,16,32,256]{3,2,1,0:T(8,128)} %u_ref.3, f32[3,16,257]{2,1,0:T(8,128)} %copy-done.1, f32[16,3,128]{2,1,0:T(4,128)} %copy-done.2, f32[16,32,256]{2,1,0:T(8,128)} %rho_ref.3, ...), custom_call_target="tpu_custom_call" | custom-call | tf_op jit(solution)/shard_map/energy/pallas_call | solution.py:274
  28.9 1.3 %collective-permute-start.5 = (f32[2,32,256]{2,1,0:T(8,128)}, f32[2,32,256]{2,1,0:T(8,128)S(1)}, u32[]{:S(2)}, u32[]{:S(2)}) collective-permute-start(f32[2,32,256]{2,1,0:T(8,128)} %get-tuple-element.20), channel_id=1, source_target_pairs={{8,0},{16,8},{24,16},{9,1},{17,9},{25,17},{10,2},{18,10},{26,18},{... | collective-permute-start | bytes 196616 | tf_op jit(solution)/shard_map/ppermute | solution.py:22
  30.8 2.7 %energy_last.1 = (f32[2,32,256]{2,1,0:T(8,128)}, f32[32,1,128]{2,1,0:T(1,128)}) custom-call(s32[3]{0:T(128)} %pad_add_fusion.where_ref, f32[3,16,32,256]{3,2,1,0:T(8,128)} %u_ref.3, f32[3,1,32,256]{3,2,1,0:T(8,128)} %copy-done.3, f32[3,512]{1,0:T(4,128)} %copy-done.7, f32[3,16,257]{2,1,0:T(8,128)} %copy-done.1, f32[16,3,128]{2,1,0:T(4,128)} %copy-done.2, ...), custom_call_target="tpu_custom_call" | custom-call | tf_op jit(solution)/shard_map/energy_last/pallas_call | solution.py:290
  33.5 4.6 %collective-permute-start.4 = (f32[2,32,256]{2,1,0:T(8,128)}, f32[2,32,256]{2,1,0:T(8,128)S(1)}, u32[]{:S(2)}, u32[]{:S(2)}) collective-permute-start(f32[2,32,256]{2,1,0:T(8,128)} %get-tuple-element.19.own_ref), channel_id=1, source_target_pairs={{0,8},{8,16},{16,24},{1,9},{9,17},{17,25},{2,10},{10,18},{18,26},{... | collective-permute-start | bytes 196616 | tf_op jit(solution)/shard_map/ppermute | solution.py:22
  38.1 1.9 %collective-permute-done.4.xlo_ref = f32[2,32,256]{2,1,0:T(8,128)S(1)} collective-permute-done((f32[2,32,256]{2,1,0:T(8,128)}, f32[2,32,256]{2,1,0:T(8,128)S(1)}, u32[]{:S(2)}, u32[]{:S(2)}) %collective-permute-start.4) | collective-permute-done | bytes 65568 | tf_op jit(solution)/shard_map/ppermute | solution.py:22
  40.0 0.6 copy-done.5
  40.6 2.0 %along_x.1 = (f32[16,32,256]{2,1,0:T(8,128)}, f32[16,2,256]{2,1,0:T(2,128)}) custom-call(s32[3]{0:T(128)} %pad_add_fusion.where_ref, f32[16,32,256]{2,1,0:T(8,128)} %get-tuple-element.17.w_ref, f32[2,32,256]{2,1,0:T(8,128)} %get-tuple-element.19.own_ref, f32[2,32,256]{2,1,0:T(8,128)} %copy-done.5, f32[2,32,256]{2,1,0:T(8,128)} %copy-done.4), custom_call_target="tpu_custom_call" | custom-call | tf_op jit(solution)/shard_map/along_x/pallas_call | solution.py:327
  42.7 15.9 %all_to_all.5 = f32[32,1,128]{2,1,0:T(1,128)S(1)} all-to-all(f32[32,1,128]{2,1,0:T(1,128)} %get-tuple-element.26), channel_id=1, replica_groups=mesh['gx'=4,'gy'=2,'gz'=4] {'gx','gy','gz'}, dimensions={0} | all-to-all | bytes 32768 | tf_op jit(solution)/shard_map/all_to_all | solution.py:316
  58.7 0.6 copy-done.6
  59.3 2.1 %along_y.1 = (f32[16,32,256]{2,1,0:T(8,128)}, f32[2,512]{1,0:T(2,128)}, f32[2,512]{1,0:T(2,128)}) custom-call(s32[3]{0:T(128)} %pad_add_fusion.where_ref, f32[16,32,256]{2,1,0:T(8,128)} %get-tuple-element.21.s_ref, f32[16,2,256]{2,1,0:T(2,128)} %copy-done.6), custom_call_target="tpu_custom_call" | custom-call | tf_op jit(solution)/shard_map/along_y/pallas_call | solution.py:332
  61.4 2.7 %collective-permute-start.7 = (f32[2,512]{1,0:T(2,128)}, f32[2,512]{1,0:T(2,128)S(1)}, u32[]{:S(2)}, u32[]{:S(2)}) collective-permute-start(f32[2,512]{1,0:T(2,128)} %get-tuple-element.24), channel_id=1, source_target_pairs={{0,1},{1,2},{2,3},{4,5},{5,6},{6,7},{8,9},{9,10},{10,11},{12,13},{... | collective-permute-start | bytes 12296 | tf_op jit(solution)/shard_map/ppermute | solution.py:22
  64.1 1.9 %collective-permute-start.8 = (f32[2,512]{1,0:T(2,128)}, f32[2,512]{1,0:T(2,128)S(1)}, u32[]{:S(2)}, u32[]{:S(2)}) collective-permute-start(f32[2,512]{1,0:T(2,128)} %get-tuple-element.25), channel_id=1, source_target_pairs={{1,0},{2,1},{3,2},{5,4},{6,5},{7,6},{9,8},{10,9},{11,10},{13,12},{... | collective-permute-start | bytes 12296 | tf_op jit(solution)/shard_map/ppermute | solution.py:22
  67.9 1.3 %collective-permute-done.8.zhi_ref = f32[2,512]{1,0:T(2,128)S(1)} collective-permute-done((f32[2,512]{1,0:T(2,128)}, f32[2,512]{1,0:T(2,128)S(1)}, u32[]{:S(2)}, u32[]{:S(2)}) %collective-permute-start.8) | collective-permute-done | bytes 4128 | tf_op jit(solution)/shard_map/ppermute | solution.py:22
  69.2 0.6 copy-done.9
  69.8 3.7 %along_z.1 = f32[16,32,256]{2,1,0:T(8,128)} custom-call(f32[16,32,256]{2,1,0:T(8,128)} %get-tuple-element.23.s_ref, f32[2,512]{1,0:T(2,128)} %copy-done.8, f32[2,512]{1,0:T(2,128)} %copy-done.9), custom_call_target="tpu_custom_call" | custom-call | tf_op jit(solution)/shard_map/along_z/pallas_call | solution.py:341
  (40 shorter events, 1.9 us)
Async XLA Ops:
  0.6 1.1 %slice-start = ((f32[3,16,32,256]{3,2,1,0:T(8,128)}), f32[3,16,32,1]{3,2,1,0:T(8,128)S(1)}, s32[]{:S(2)}) async-start(f32[3,16,32,256]{3,2,1,0:T(8,128)} %u_ref.3), calls=%async_computation.1 | async-start | bytes 1572864 | tf_op jit(solution)/shard_map/slice | solution.py:254
  0.6 3.5 %copy-start = (f32[3,16,32,256]{3,2,1,0:T(8,128)S(1)}, f32[3,16,32,256]{3,2,1,0:T(8,128)}, u32[]{:S(2)}) copy-start(f32[3,16,32,256]{3,2,1,0:T(8,128)} %u_ref.3) | copy-start | bytes 4718596
  2.2 6.1 %collective-permute-start = (f32[16,3,128]{2,1,0:T(4,128)S(1)}, f32[16,3,128]{2,1,0:T(4,128)S(1)}, u32[]{:S(2)}, u32[]{:S(2)}) collective-permute-start(f32[16,3,128]{2,1,0:T(4,128)S(1)} %pad.4), channel_id=1, source_target_pairs={{1,0},{2,1},{3,2},{5,4},{6,5},{7,6},{9,8},{10,9},{11,10},{13,12},{... | collective-permute-start | bytes 73736 | tf_op jit(solution)/shard_map/ppermute | solution.py:22
  4.2 26.0 %collective-permute-start.2 = (f32[3,1,32,256]{3,2,1,0:T(8,128)S(1)}, f32[3,1,32,256]{3,2,1,0:T(8,128)S(1)}, u32[]{:S(2)}, u32[]{:S(2)}) collective-permute-start(f32[3,1,32,256]{3,2,1,0:T(8,128)S(1)} %slice.27), channel_id=1, source_target_pairs={{8,0},{16,8},{24,16},{9,1},{17,9},{25,17},{10,2},{18,10},{26,18},{... | collective-permute-start | bytes 294920 | tf_op jit(solution)/shard_map/ppermute | solution.py:22
  8.3 8.8 %copy-start.2 = (f32[16,3,128]{2,1,0:T(4,128)}, f32[16,3,128]{2,1,0:T(4,128)S(1)}, u32[]{:S(2)}) copy-start(f32[16,3,128]{2,1,0:T(4,128)S(1)} %collective-permute-done.zh_ref) | copy-start | bytes 73732
  8.4 5.1 %collective-permute-start.1 = (f32[3,16,257]{2,1,0:T(8,128)S(1)}, f32[3,16,257]{2,1,0:T(8,128)S(1)}, u32[]{:S(2)}, u32[]{:S(2)}) collective-permute-start(f32[3,16,257]{2,1,0:T(8,128)S(1)} %pad_maximum_fusion), channel_id=1, source_target_pairs={{4,0},{5,1},{6,2},{7,3},{12,8},{13,9},{14,10},{15,11},{20,16},{21,... | collective-permute-start | bytes 148040 | tf_op jit(solution)/shard_map/ppermute | solution.py:22
  13.5 3.7 %copy-start.1 = (f32[3,16,257]{2,1,0:T(8,128)}, f32[3,16,257]{2,1,0:T(8,128)S(1)}, u32[]{:S(2)}) copy-start(f32[3,16,257]{2,1,0:T(8,128)S(1)} %collective-permute-done.1.yh_ref) | copy-start | bytes 148036
  13.5 16.7 %collective-permute-start.3 = (f32[3,512]{1,0:T(4,128)S(1)}, f32[3,512]{1,0:T(4,128)S(1)}, u32[]{:S(2)}, u32[]{:S(2)}) collective-permute-start(f32[3,512]{1,0:T(4,128)S(1)} %pad_maximum_fusion.1), channel_id=1, source_target_pairs={{8,0},{16,8},{24,16},{9,1},{17,9},{25,17},{10,2},{18,10},{26,18},{... | collective-permute-start | bytes 18440 | tf_op jit(solution)/shard_map/ppermute | solution.py:22
  28.9 9.2 %collective-permute-start.5 = (f32[2,32,256]{2,1,0:T(8,128)}, f32[2,32,256]{2,1,0:T(8,128)S(1)}, u32[]{:S(2)}, u32[]{:S(2)}) collective-permute-start(f32[2,32,256]{2,1,0:T(8,128)} %get-tuple-element.20), channel_id=1, source_target_pairs={{8,0},{16,8},{24,16},{9,1},{17,9},{25,17},{10,2},{18,10},{26,18},{... | collective-permute-start | bytes 196616 | tf_op jit(solution)/shard_map/ppermute | solution.py:22
  30.2 0.6 copy-start.7
  30.2 0.6 copy-start.3
  33.5 6.5 %collective-permute-start.4 = (f32[2,32,256]{2,1,0:T(8,128)}, f32[2,32,256]{2,1,0:T(8,128)S(1)}, u32[]{:S(2)}, u32[]{:S(2)}) collective-permute-start(f32[2,32,256]{2,1,0:T(8,128)} %get-tuple-element.19.own_ref), channel_id=1, source_target_pairs={{0,8},{8,16},{16,24},{1,9},{9,17},{17,25},{2,10},{10,18},{18,26},{... | collective-permute-start | bytes 196616 | tf_op jit(solution)/shard_map/ppermute | solution.py:22
  38.1 1.9 %copy-start.4 = (f32[2,32,256]{2,1,0:T(8,128)}, f32[2,32,256]{2,1,0:T(8,128)S(1)}, u32[]{:S(2)}) copy-start(f32[2,32,256]{2,1,0:T(8,128)S(1)} %collective-permute-done.5.xhi_ref) | copy-start | bytes 196612
  40.0 0.6 copy-start.5
  42.7 16.0 %collective-permute-start.6 = (f32[16,2,256]{2,1,0:T(2,128)}, f32[16,2,256]{2,1,0:T(2,128)S(1)}, u32[]{:S(2)}, u32[]{:S(2)}) collective-permute-start(f32[16,2,256]{2,1,0:T(2,128)} %get-tuple-element.22), channel_id=1, source_target_pairs={{0,4},{4,0},{1,5},{5,1},{2,6},{6,2},{3,7},{7,3},{8,12},{12,8},{9,1... | collective-permute-start | bytes 98312 | tf_op jit(solution)/shard_map/ppermute | solution.py:329
  58.7 0.6 copy-start.6
  61.4 6.5 %collective-permute-start.7 = (f32[2,512]{1,0:T(2,128)}, f32[2,512]{1,0:T(2,128)S(1)}, u32[]{:S(2)}, u32[]{:S(2)}) collective-permute-start(f32[2,512]{1,0:T(2,128)} %get-tuple-element.24), channel_id=1, source_target_pairs={{0,1},{1,2},{2,3},{4,5},{5,6},{6,7},{8,9},{9,10},{10,11},{12,13},{... | collective-permute-start | bytes 12296 | tf_op jit(solution)/shard_map/ppermute | solution.py:22
  64.1 5.1 %collective-permute-start.8 = (f32[2,512]{1,0:T(2,128)}, f32[2,512]{1,0:T(2,128)S(1)}, u32[]{:S(2)}, u32[]{:S(2)}) collective-permute-start(f32[2,512]{1,0:T(2,128)} %get-tuple-element.25), channel_id=1, source_target_pairs={{1,0},{2,1},{3,2},{5,4},{6,5},{7,6},{9,8},{10,9},{11,10},{13,12},{... | collective-permute-start | bytes 12296 | tf_op jit(solution)/shard_map/ppermute | solution.py:22
  67.9 1.3 %copy-start.8 = (f32[2,512]{1,0:T(2,128)}, f32[2,512]{1,0:T(2,128)S(1)}, u32[]{:S(2)}) copy-start(f32[2,512]{1,0:T(2,128)S(1)} %collective-permute-done.7.zlo_ref) | copy-start | bytes 12292
  69.2 0.6 copy-start.9

commit v5 on v4

--- a/solution.py
+++ b/solution.py
@@ -101,15 +101,22 @@
 
 def main_kernel(
     where_ref, u_ref, yh_ref, zh_ref, rho_ref, gains, inv_ref, w_ref, low_ref, sums_ref, corners,
-    *, extent
+    nodes, arrived, *, extent
 ):
     planes, _, length = rho_ref.shape
 
+    def fetch(p):
+        return pltpu.make_async_copy(u_ref.at[:, p], nodes.at[:, p], arrived.at[p])
+
+    for p in range(planes):
+        fetch(p).start()
+
     def load(p, slot):
+        fetch(p).wait()
         prepare(
             corners,
             slot,
-            lambda m: u_ref[m, p],
+            lambda m: nodes[m, p],
             lambda m, c: yh_ref[m, pl.ds(p, 1), c : c + length],
             zh_ref[p],
         )
@@ -273,10 +280,14 @@
     corner_space = pltpu.VMEM((2, 12, height, length), F32)
     weighted, low, part = pl.pallas_call(
         functools.partial(main_kernel, extent=extents[0]),
-        in_specs=[SMEM] + [VMEM] * 6,
+        in_specs=[SMEM, pl.BlockSpec(memory_space=pl.ANY)] + [VMEM] * 5,
         out_specs=[VMEM] * 3,
         out_shape=[shape(planes, height, length), shape(2, height, length), shape(2, ROWS, length)],
-        scratch_shapes=[corner_space],
+        scratch_shapes=[
+            corner_space,
+            pltpu.VMEM((3, planes, height, length), F32),
+            pltpu.SemaphoreType.DMA((planes,)),
+        ],
         name="energy",
     )(where, displacement, yh, zh, density, gains, inverse)
     xhi = shift_from(low, "gx", 1)

time: 76.3 us -> 79.1 us (1.037)
  Pallas kernels: 24 us -> 26.7 us
    pallas_call x1, Pallas kernels: 11.7 us -> 14.4 us  [on_device(): pl.pallas_call(functools.partial(main_kernel, extent=extents[0]), in_spec...]
  transfers between devices with their start and end apart: 9 -> 9, of which waited for: 4 -> 4; matrix products, arithmetic and copies ran while one was open for 2% -> 2% of each run, Pallas kernels for 21% -> 24%
where the time goes in v5:
time: 79.1 us; the launch traced here: 78.5 us
  Pallas kernels  26.7 us (34%)
  starting transfers between devices  16.3 us (21%)
  blocking collectives  15.9 us (20%)
  waiting for transfers between devices  9.66 us (12%)
  local copies, waits for them, and re-layouts  4.78 us (6%)
  between operations  4.46 us (6%)
    ppermute x8, starting transfers between devices, shift_from(): return lax.ppermute(block, axis, route)  16.3 us
    all_to_all x1, blocking collectives, on_device(): gathered = lax.all_to_all(sums, AXES, 0, 0, tiled=True)  15.9 us
    pallas_call x1, Pallas kernels, on_device(): pl.pallas_call(functools.partial(main_kernel, extent=extents[0]), in_spec...  14.4 us
    ppermute x8, waiting for transfers between devices, shift_from(): return lax.ppermute(block, axis, route)  9.66 us
    pallas_call x1, Pallas kernels, on_device(): pl.pallas_call(third_kernel, in_specs=[VMEM] * 3, out_specs=VMEM, out_sha...  3.7 us
    unnamed x23, local copies, waits for them, and re-layouts  2.93 us
    pallas_call x1, Pallas kernels, on_device(): pl.pallas_call(functools.partial(last_kernel, extent=extents[0], planes=p...  2.65 us
    pallas_call x1, Pallas kernels, on_device(): pl.pallas_call(second_kernel, in_specs=[SMEM] + [VMEM] * (1 + rows), out_...  2.13 us
  transfers between devices with their start and end apart: 9, of which 4 were waited for; matrix products, arithmetic and copies ran while one was open for 2% of the time, Pallas kernels for 24%

profile of v5, /device:TPU:1, one launch (start us, length us, event | category | flops | bytes accessed | tf_op | source)
XLA Modules:
  0.0 78.5 jit_solution(17709126985841707678)
XLA Ops:
  0.7 1.1 %slice-done = f32[3,16,32,1]{3,2,1,0:T(8,128)S(1)} async-done(((f32[3,16,32,256]{3,2,1,0:T(8,128)}), f32[3,16,32,1]{3,2,1,0:T(8,128)S(1)}, s32[]{:S(2)}) %slice-start) | async-done | bytes 6168 | tf_op jit(solution)/shard_map/slice | solution.py:261
  2.2 1.9 %collective-permute-start = (f32[16,3,128]{2,1,0:T(4,128)S(1)}, f32[16,3,128]{2,1,0:T(4,128)S(1)}, u32[]{:S(2)}, u32[]{:S(2)}) collective-permute-start(f32[16,3,128]{2,1,0:T(4,128)S(1)} %pad.4), channel_id=1, source_target_pairs={{1,0},{2,1},{3,2},{5,4},{6,5},{7,6},{9,8},{10,9},{11,10},{13,12},{... | collective-permute-start | bytes 73736 | tf_op jit(solution)/shard_map/ppermute | solution.py:22
  4.2 1.3 %collective-permute-start.2 = (f32[3,1,32,256]{3,2,1,0:T(8,128)S(1)}, f32[3,1,32,256]{3,2,1,0:T(8,128)S(1)}, u32[]{:S(2)}, u32[]{:S(2)}) collective-permute-start(f32[3,1,32,256]{3,2,1,0:T(8,128)S(1)} %slice.27), channel_id=1, source_target_pairs={{8,0},{16,8},{24,16},{9,1},{17,9},{25,17},{10,2},{18,10},{26,18},{... | collective-permute-start | bytes 294920 | tf_op jit(solution)/shard_map/ppermute | solution.py:22
  5.6 2.7 %collective-permute-done.zh_ref = f32[16,3,128]{2,1,0:T(4,128)S(1)} collective-permute-done((f32[16,3,128]{2,1,0:T(4,128)S(1)}, f32[16,3,128]{2,1,0:T(4,128)S(1)}, u32[]{:S(2)}, u32[]{:S(2)}) %collective-permute-start) | collective-permute-done | bytes 24608 | tf_op jit(solution)/shard_map/ppermute | solution.py:22
  8.4 1.3 %collective-permute-start.1 = (f32[3,16,257]{2,1,0:T(8,128)S(1)}, f32[3,16,257]{2,1,0:T(8,128)S(1)}, u32[]{:S(2)}, u32[]{:S(2)}) collective-permute-start(f32[3,16,257]{2,1,0:T(8,128)S(1)} %pad_maximum_fusion), channel_id=1, source_target_pairs={{4,0},{5,1},{6,2},{7,3},{12,8},{13,9},{14,10},{15,11},{20,16},{21,... | collective-permute-start | bytes 148040 | tf_op jit(solution)/shard_map/ppermute | solution.py:22
  9.7 3.8 %collective-permute-done.1.yh_ref = f32[3,16,257]{2,1,0:T(8,128)S(1)} collective-permute-done((f32[3,16,257]{2,1,0:T(8,128)S(1)}, f32[3,16,257]{2,1,0:T(8,128)S(1)}, u32[]{:S(2)}, u32[]{:S(2)}) %collective-permute-start.1) | collective-permute-done | bytes 49376 | tf_op jit(solution)/shard_map/ppermute | solution.py:22
  13.5 1.3 %collective-permute-start.3 = (f32[3,512]{1,0:T(4,128)S(1)}, f32[3,512]{1,0:T(4,128)S(1)}, u32[]{:S(2)}, u32[]{:S(2)}) collective-permute-start(f32[3,512]{1,0:T(4,128)S(1)} %pad_maximum_fusion.1), channel_id=1, source_target_pairs={{8,0},{16,8},{24,16},{9,1},{17,9},{25,17},{10,2},{18,10},{26,18},{... | collective-permute-start | bytes 18440 | tf_op jit(solution)/shard_map/ppermute | solution.py:22
  14.8 0.7 pad_add_fusion.where_ref
  15.4 1.7 %setup.1 = (bf16[384,192]{1,0:T(8,128)(2,1)}, f32[32,256]{1,0:T(8,128)}) custom-call(s32[3]{0:T(128)} %pad_add_fusion.where_ref, f32[24,24]{1,0:T(8,128)} %k_ref.1), custom_call_target="tpu_custom_call" | custom-call | tf_op jit(solution)/shard_map/setup/pallas_call | solution.py:279
  17.2 14.4 %energy.1 = (f32[16,32,256]{2,1,0:T(8,128)}, f32[2,32,256]{2,1,0:T(8,128)}, f32[2,8,256]{2,1,0:T(8,128)}) custom-call(s32[3]{0:T(128)} %pad_add_fusion.where_ref, f32[3,16,32,256]{3,2,1,0:T(8,128)} %u_ref.3, f32[3,16,257]{2,1,0:T(8,128)} %copy-done.1, f32[16,3,128]{2,1,0:T(4,128)} %copy-done.2, f32[16,32,256]{2,1,0:T(8,128)} %rho_ref.3, ...), custom_call_target="tpu_custom_call" | custom-call | tf_op jit(solution)/shard_map/energy/pallas_call | solution.py:281
  31.6 1.3 %collective-permute-start.5 = (f32[2,32,256]{2,1,0:T(8,128)}, f32[2,32,256]{2,1,0:T(8,128)S(1)}, u32[]{:S(2)}, u32[]{:S(2)}) collective-permute-start(f32[2,32,256]{2,1,0:T(8,128)} %get-tuple-element.20), channel_id=1, source_target_pairs={{8,0},{16,8},{24,16},{9,1},{17,9},{25,17},{10,2},{18,10},{26,18},{... | collective-permute-start | bytes 196616 | tf_op jit(solution)/shard_map/ppermute | solution.py:22
  33.6 2.7 %energy_last.1 = (f32[2,32,256]{2,1,0:T(8,128)}, f32[32,1,128]{2,1,0:T(1,128)}) custom-call(s32[3]{0:T(128)} %pad_add_fusion.where_ref, f32[3,16,32,256]{3,2,1,0:T(8,128)} %u_ref.3, f32[3,1,32,256]{3,2,1,0:T(8,128)} %copy-done.3, f32[3,512]{1,0:T(4,128)} %copy-done.7, f32[3,16,257]{2,1,0:T(8,128)} %copy-done.1, f32[16,3,128]{2,1,0:T(4,128)} %copy-done.2, ...), custom_call_target="tpu_custom_call" | custom-call | tf_op jit(solution)/shard_map/energy_last/pallas_call | solution.py:301
  36.2 4.6 %collective-permute-start.4 = (f32[2,32,256]{2,1,0:T(8,128)}, f32[2,32,256]{2,1,0:T(8,128)S(1)}, u32[]{:S(2)}, u32[]{:S(2)}) collective-permute-start(f32[2,32,256]{2,1,0:T(8,128)} %get-tuple-element.19.own_ref), channel_id=1, source_target_pairs={{0,8},{8,16},{16,24},{1,9},{9,17},{17,25},{2,10},{10,18},{18,26},{... | collective-permute-start | bytes 196616 | tf_op jit(solution)/shard_map/ppermute | solution.py:22
  40.9 1.9 %collective-permute-done.4.xlo_ref = f32[2,32,256]{2,1,0:T(8,128)S(1)} collective-permute-done((f32[2,32,256]{2,1,0:T(8,128)}, f32[2,32,256]{2,1,0:T(8,128)S(1)}, u32[]{:S(2)}, u32[]{:S(2)}) %collective-permute-start.4) | collective-permute-done | bytes 65568 | tf_op jit(solution)/shard_map/ppermute | solution.py:22
  42.7 0.6 copy-done.5
  43.4 2.0 %along_x.1 = (f32[16,32,256]{2,1,0:T(8,128)}, f32[16,2,256]{2,1,0:T(2,128)}) custom-call(s32[3]{0:T(128)} %pad_add_fusion.where_ref, f32[16,32,256]{2,1,0:T(8,128)} %get-tuple-element.17.w_ref, f32[2,32,256]{2,1,0:T(8,128)} %get-tuple-element.19.own_ref, f32[2,32,256]{2,1,0:T(8,128)} %copy-done.5, f32[2,32,256]{2,1,0:T(8,128)} %copy-done.4), custom_call_target="tpu_custom_call" | custom-call | tf_op jit(solution)/shard_map/along_x/pallas_call | solution.py:338
  45.4 15.9 %all_to_all.5 = f32[32,1,128]{2,1,0:T(1,128)S(1)} all-to-all(f32[32,1,128]{2,1,0:T(1,128)} %get-tuple-element.26), channel_id=1, replica_groups=mesh['gx'=4,'gy'=2,'gz'=4] {'gx','gy','gz'}, dimensions={0} | all-to-all | bytes 32768 | tf_op jit(solution)/shard_map/all_to_all | solution.py:327
  61.4 0.6 copy-done.6
  62.0 2.1 %along_y.1 = (f32[16,32,256]{2,1,0:T(8,128)}, f32[2,512]{1,0:T(2,128)}, f32[2,512]{1,0:T(2,128)}) custom-call(s32[3]{0:T(128)} %pad_add_fusion.where_ref, f32[16,32,256]{2,1,0:T(8,128)} %get-tuple-element.21.s_ref, f32[16,2,256]{2,1,0:T(2,128)} %copy-done.6), custom_call_target="tpu_custom_call" | custom-call | tf_op jit(solution)/shard_map/along_y/pallas_call | solution.py:343
  64.1 2.7 %collective-permute-start.7 = (f32[2,512]{1,0:T(2,128)}, f32[2,512]{1,0:T(2,128)S(1)}, u32[]{:S(2)}, u32[]{:S(2)}) collective-permute-start(f32[2,512]{1,0:T(2,128)} %get-tuple-element.24), channel_id=1, source_target_pairs={{0,1},{1,2},{2,3},{4,5},{5,6},{6,7},{8,9},{9,10},{10,11},{12,13},{... | collective-permute-start | bytes 12296 | tf_op jit(solution)/shard_map/ppermute | solution.py:22
  66.8 1.9 %collective-permute-start.8 = (f32[2,512]{1,0:T(2,128)}, f32[2,512]{1,0:T(2,128)S(1)}, u32[]{:S(2)}, u32[]{:S(2)}) collective-permute-start(f32[2,512]{1,0:T(2,128)} %get-tuple-element.25), channel_id=1, source_target_pairs={{1,0},{2,1},{3,2},{5,4},{6,5},{7,6},{9,8},{10,9},{11,10},{13,12},{... | collective-permute-start | bytes 12296 | tf_op jit(solution)/shard_map/ppermute | solution.py:22
  70.7 1.3 %collective-permute-done.8.zhi_ref = f32[2,512]{1,0:T(2,128)S(1)} collective-permute-done((f32[2,512]{1,0:T(2,128)}, f32[2,512]{1,0:T(2,128)S(1)}, u32[]{:S(2)}, u32[]{:S(2)}) %collective-permute-start.8) | collective-permute-done | bytes 4128 | tf_op jit(solution)/shard_map/ppermute | solution.py:22
  72.0 0.6 copy-done.9
  72.6 3.7 %along_z.1 = f32[16,32,256]{2,1,0:T(8,128)} custom-call(f32[16,32,256]{2,1,0:T(8,128)} %get-tuple-element.23.s_ref, f32[2,512]{1,0:T(2,128)} %copy-done.8, f32[2,512]{1,0:T(2,128)} %copy-done.9), custom_call_target="tpu_custom_call" | custom-call | tf_op jit(solution)/shard_map/along_z/pallas_call | solution.py:352
  (40 shorter events, 1.9 us)
Async XLA Ops:
  0.6 1.1 %slice-start = ((f32[3,16,32,256]{3,2,1,0:T(8,128)}), f32[3,16,32,1]{3,2,1,0:T(8,128)S(1)}, s32[]{:S(2)}) async-start(f32[3,16,32,256]{3,2,1,0:T(8,128)} %u_ref.3), calls=%async_computation.1 | async-start | bytes 1572864 | tf_op jit(solution)/shard_map/slice | solution.py:261
  0.6 3.5 %copy-start = (f32[3,16,32,256]{3,2,1,0:T(8,128)S(1)}, f32[3,16,32,256]{3,2,1,0:T(8,128)}, u32[]{:S(2)}) copy-start(f32[3,16,32,256]{3,2,1,0:T(8,128)} %u_ref.3) | copy-start | bytes 4718596
  2.2 6.1 %collective-permute-start = (f32[16,3,128]{2,1,0:T(4,128)S(1)}, f32[16,3,128]{2,1,0:T(4,128)S(1)}, u32[]{:S(2)}, u32[]{:S(2)}) collective-permute-start(f32[16,3,128]{2,1,0:T(4,128)S(1)} %pad.4), channel_id=1, source_target_pairs={{1,0},{2,1},{3,2},{5,4},{6,5},{7,6},{9,8},{10,9},{11,10},{13,12},{... | collective-permute-start | bytes 73736 | tf_op jit(solution)/shard_map/ppermute | solution.py:22
  4.2 28.7 %collective-permute-start.2 = (f32[3,1,32,256]{3,2,1,0:T(8,128)S(1)}, f32[3,1,32,256]{3,2,1,0:T(8,128)S(1)}, u32[]{:S(2)}, u32[]{:S(2)}) collective-permute-start(f32[3,1,32,256]{3,2,1,0:T(8,128)S(1)} %slice.27), channel_id=1, source_target_pairs={{8,0},{16,8},{24,16},{9,1},{17,9},{25,17},{10,2},{18,10},{26,18},{... | collective-permute-start | bytes 294920 | tf_op jit(solution)/shard_map/ppermute | solution.py:22
  8.3 8.8 %copy-start.2 = (f32[16,3,128]{2,1,0:T(4,128)}, f32[16,3,128]{2,1,0:T(4,128)S(1)}, u32[]{:S(2)}) copy-start(f32[16,3,128]{2,1,0:T(4,128)S(1)} %collective-permute-done.zh_ref) | copy-start | bytes 73732
  8.4 5.1 %collective-permute-start.1 = (f32[3,16,257]{2,1,0:T(8,128)S(1)}, f32[3,16,257]{2,1,0:T(8,128)S(1)}, u32[]{:S(2)}, u32[]{:S(2)}) collective-permute-start(f32[3,16,257]{2,1,0:T(8,128)S(1)} %pad_maximum_fusion), channel_id=1, source_target_pairs={{4,0},{5,1},{6,2},{7,3},{12,8},{13,9},{14,10},{15,11},{20,16},{21,... | collective-permute-start | bytes 148040 | tf_op jit(solution)/shard_map/ppermute | solution.py:22
  13.5 3.7 %copy-start.1 = (f32[3,16,257]{2,1,0:T(8,128)}, f32[3,16,257]{2,1,0:T(8,128)S(1)}, u32[]{:S(2)}) copy-start(f32[3,16,257]{2,1,0:T(8,128)S(1)} %collective-permute-done.1.yh_ref) | copy-start | bytes 148036
  13.5 19.4 %collective-permute-start.3 = (f32[3,512]{1,0:T(4,128)S(1)}, f32[3,512]{1,0:T(4,128)S(1)}, u32[]{:S(2)}, u32[]{:S(2)}) collective-permute-start(f32[3,512]{1,0:T(4,128)S(1)} %pad_maximum_fusion.1), channel_id=1, source_target_pairs={{8,0},{16,8},{24,16},{9,1},{17,9},{25,17},{10,2},{18,10},{26,18},{... | collective-permute-start | bytes 18440 | tf_op jit(solution)/shard_map/ppermute | solution.py:22
  31.6 9.2 %collective-permute-start.5 = (f32[2,32,256]{2,1,0:T(8,128)}, f32[2,32,256]{2,1,0:T(8,128)S(1)}, u32[]{:S(2)}, u32[]{:S(2)}) collective-permute-start(f32[2,32,256]{2,1,0:T(8,128)} %get-tuple-element.20), channel_id=1, source_target_pairs={{8,0},{16,8},{24,16},{9,1},{17,9},{25,17},{10,2},{18,10},{26,18},{... | collective-permute-start | bytes 196616 | tf_op jit(solution)/shard_map/ppermute | solution.py:22
  32.9 0.6 copy-start.7
  32.9 0.6 copy-start.3
  36.2 6.5 %collective-permute-start.4 = (f32[2,32,256]{2,1,0:T(8,128)}, f32[2,32,256]{2,1,0:T(8,128)S(1)}, u32[]{:S(2)}, u32[]{:S(2)}) collective-permute-start(f32[2,32,256]{2,1,0:T(8,128)} %get-tuple-element.19.own_ref), channel_id=1, source_target_pairs={{0,8},{8,16},{16,24},{1,9},{9,17},{17,25},{2,10},{10,18},{18,26},{... | collective-permute-start | bytes 196616 | tf_op jit(solution)/shard_map/ppermute | solution.py:22
  40.8 1.9 %copy-start.4 = (f32[2,32,256]{2,1,0:T(8,128)}, f32[2,32,256]{2,1,0:T(8,128)S(1)}, u32[]{:S(2)}) copy-start(f32[2,32,256]{2,1,0:T(8,128)S(1)} %collective-permute-done.5.xhi_ref) | copy-start | bytes 196612
  42.7 0.6 copy-start.5
  45.4 16.0 %collective-permute-start.6 = (f32[16,2,256]{2,1,0:T(2,128)}, f32[16,2,256]{2,1,0:T(2,128)S(1)}, u32[]{:S(2)}, u32[]{:S(2)}) collective-permute-start(f32[16,2,256]{2,1,0:T(2,128)} %get-tuple-element.22), channel_id=1, source_target_pairs={{0,4},{4,0},{1,5},{5,1},{2,6},{6,2},{3,7},{7,3},{8,12},{12,8},{9,1... | collective-permute-start | bytes 98312 | tf_op jit(solution)/shard_map/ppermute | solution.py:340
  61.4 0.6 copy-start.6
  64.1 6.5 %collective-permute-start.7 = (f32[2,512]{1,0:T(2,128)}, f32[2,512]{1,0:T(2,128)S(1)}, u32[]{:S(2)}, u32[]{:S(2)}) collective-permute-start(f32[2,512]{1,0:T(2,128)} %get-tuple-element.24), channel_id=1, source_target_pairs={{0,1},{1,2},{2,3},{4,5},{5,6},{6,7},{8,9},{9,10},{10,11},{12,13},{... | collective-permute-start | bytes 12296 | tf_op jit(solution)/shard_map/ppermute | solution.py:22
  66.8 5.1 %collective-permute-start.8 = (f32[2,512]{1,0:T(2,128)}, f32[2,512]{1,0:T(2,128)S(1)}, u32[]{:S(2)}, u32[]{:S(2)}) collective-permute-start(f32[2,512]{1,0:T(2,128)} %get-tuple-element.25), channel_id=1, source_target_pairs={{1,0},{2,1},{3,2},{5,4},{6,5},{7,6},{9,8},{10,9},{11,10},{13,12},{... | collective-permute-start | bytes 12296 | tf_op jit(solution)/shard_map/ppermute | solution.py:22
  70.6 1.3 %copy-start.8 = (f32[2,512]{1,0:T(2,128)}, f32[2,512]{1,0:T(2,128)S(1)}, u32[]{:S(2)}) copy-start(f32[2,512]{1,0:T(2,128)S(1)} %collective-permute-done.7.zlo_ref) | copy-start | bytes 12292
  72.0 0.6 copy-start.9
